TPU v7x, 32 devices: a whole 2x2x4 slice. The times are simulated.
32 devices in a mesh: rows: 4 (over y, x), cols: 8 (over z, core).
Axes of the slice: x: 2, y: 2, z: 4, core: 2. Of those that a mesh axis runs over, the one named last changes fastest.
Arguments:
- factor_u: float32 [4, 2048, 128], P('rows', 'cols'), may hold values from -2 to 2
- factor_v: float32 [8, 512, 128], P('cols', 'rows'), may hold values from -2 to 2
- values: bfloat16 [4, 8, 8, 256, 256], P('rows', 'cols'), may hold values from -6 to 6
- mask_words: int32 [4, 8, 8, 16, 256], P('rows', 'cols'), may hold values from 0 to 65535, as said below
- tile_cols: int32 [4, 8, 8], P('rows', 'cols'), may hold values from 0 to 1
Outputs:
- new_u: float32 [4, 2048, 128], P('rows', 'cols')
- new_v: float32 [8, 512, 128], P('cols', 'rows')
- loss: float32 [], replicated
Inputs may be any that keep to these rules, and one draw needn't show every extreme that they name: `mask_words`: bit b of word w of a slot marks the entry in row 16 w + b of the tile.
All inputs are finite; a program needn't handle non-finite values.
Results may differ from a plain program's by a relative error of at most 0.02.
Values may be sent and summed in bfloat16 or wider, within the bound.
No kernel may reach another device: no remote copies, remote signals or barrier semaphores. Data moves between devices by JAX's collectives and lax.ppermute only.
A program may use at most 64 MiB of HBM per device.

v0:
```python
import functools

import jax
import jax.numpy as jnp
from jax import lax
from jax.experimental import pallas as pl
from jax.experimental.pallas import tpu as pltpu
from jax.sharding import PartitionSpec as P


step_rate = 0.01
ridge_weight = 0.1
bf16 = jnp.bfloat16
f32 = jnp.float32
LOSS_ROWS = 16
WORD_BITS = 16
VMEM_LIMIT = 24 * 2**20
sds = jax.ShapeDtypeStruct


def partners(size, bit):
    return [(i, i ^ bit) for i in range(size)]


def far_order(n_cols):
    return sorted(range(2, n_cols, 2), key=lambda q: (q != 4, -q))


def row_order(n_rows):
    return list(range(1, n_rows))


def call(body, out_shape, args, scratch=(), spaces=None, flops=0):
    spaces = spaces or {}
    specs = [pl.BlockSpec(memory_space=spaces.get(i, pltpu.VMEM)) for i in range(len(args))]
    return pl.pallas_call(
        body,
        out_shape=out_shape,
        in_specs=specs,
        out_specs=jax.tree.map(lambda _: pl.BlockSpec(memory_space=pltpu.VMEM), out_shape),
        scratch_shapes=list(scratch),
        compiler_params=pltpu.CompilerParams(vmem_limit_bytes=VMEM_LIMIT),
        cost_estimate=pl.CostEstimate(flops=flops, bytes_accessed=0, transcendentals=0),
    )(*args)


def pack_loss(loss_row):
    width = loss_row.shape[-1]
    hi = loss_row.astype(bf16).astype(f32)
    mid = (loss_row - hi).astype(bf16).astype(f32)
    lo = loss_row - hi - mid
    which = lax.broadcasted_iota(jnp.int32, (LOSS_ROWS, width), 0)
    rows = jnp.where(which == 0, hi, jnp.where(which == 1, mid, jnp.where(which == 2, lo, 0.0)))
    return rows.astype(bf16)


def read_loss(block):
    rows = block[...].astype(f32)
    return rows[0:1] + rows[1:2] + rows[2:3]


def fetch_kernel(*refs):
    count = len(refs) // 2
    sems = refs[-1]
    copies = [
        pltpu.make_async_copy(refs[i], refs[count + i], sems.at[i]) for i in range(count)
    ]
    for copy in copies:
        copy.start()
    for copy in copies:
        copy.wait()


def tile_kernel(n_cols, n_rows, tile, *refs):
    column_ids, values, words, own_u, own_v = refs[:5]
    u_blocks = refs[5 : 5 + n_cols]
    v_blocks = refs[5 + n_cols : 5 + n_cols + n_rows]
    low_out, v_band, *v_parts, v_total = refs[5 + n_cols + n_rows :]
    col = lax.axis_index("cols")
    row = lax.axis_index("rows")
    v_rows = own_v.shape[0]
    for q in range(n_rows):
        v_band[pl.ds((row ^ q) * v_rows, v_rows), :] = v_blocks[q][...]
    v_total[...] = jnp.zeros_like(v_total)
    block_rows = u_blocks[0].shape[0]
    bit = jnp.left_shift(1, lax.broadcasted_iota(jnp.int32, (WORD_BITS, tile), 0))
    squares = jnp.zeros((8, tile), f32)
    tiles = block_rows // tile
    for q in range(n_cols):
        for t in range(tiles):
            slot = (col ^ q) * tiles + t
            start = column_ids[slot] * tile
            left = u_blocks[q][t * tile : (t + 1) * tile, :]
            right = v_band[pl.ds(start, tile), :]
            predicted = lax.dot_general(
                left, right, (((1,), (1,)), ((), ())), preferred_element_type=f32
            )
            diff = predicted - values[slot].astype(f32)
            parts = []
            for w in range(tile // WORD_BITS):
                marks = jnp.broadcast_to(words[slot, w : w + 1, :], (WORD_BITS, tile))
                seen = jnp.bitwise_and(marks, bit) != 0
                parts.append(jnp.where(seen, diff[w * WORD_BITS : (w + 1) * WORD_BITS, :], 0.0))
            residual = jnp.concatenate(parts, axis=0)
            squares += jnp.sum((residual * residual).reshape(-1, 8, tile), axis=0)
            low = residual.astype(bf16)
            low_out[q * tiles + t] = low
            v_total[pl.ds(start, tile), :] += lax.dot_general(
                low, left, (((0,), (0,)), ((), ())), preferred_element_type=f32
            )
    u_own = own_u[...]
    v_own = own_v[...]
    loss = 0.5 * jnp.sum(squares) + 0.5 * ridge_weight * (
        jnp.sum(u_own * u_own) + jnp.sum(v_own * v_own)
    )
    packed = pack_loss(jnp.full((1, v_band.shape[-1]), loss, f32))
    for q in range(n_rows):
        v_parts[q][:v_rows, :] = v_total[pl.ds((row ^ q) * v_rows, v_rows), :].astype(bf16)
        v_parts[q][v_rows:, :] = packed


def rows_kernel(n_cols, tile, column_ids, low, v_band, same, cross):
    col = lax.axis_index("cols")
    tiles = low.shape[0] // n_cols
    for q in range(n_cols):
        target = cross if q & 1 else same
        for t in range(tiles):
            start = column_ids[(col ^ q) * tiles + t] * tile
            grad = jnp.dot(
                low[q * tiles + t], v_band[pl.ds(start, tile), :], preferred_element_type=f32
            )
            target[q // 2, t * tile : (t + 1) * tile, :] = grad.astype(bf16)


def v_sum_kernel(*refs):
    parts, (total_out, loss_out) = refs[:-2], refs[-2:]
    v_rows = total_out.shape[0]
    total = parts[0][:v_rows, :].astype(f32)
    loss = read_loss(parts[0].at[v_rows:])
    for part in parts[1:]:
        total += part[:v_rows, :].astype(f32)
        loss += read_loss(part.at[v_rows:])
    total_out[...] = total
    loss_out[...] = jnp.broadcast_to(loss, loss_out.shape)


def carry_kernel(loss, loss_other, same, got, *outs):
    total = loss[0:1] + loss_other[0:1]
    packed = pack_loss(total)
    rows = same.shape[1]
    for q, out in enumerate(outs):
        out[:rows, :] = (same[q].astype(f32) + got[q].astype(f32)).astype(bf16)
        out[rows:, :] = packed


def v_new_kernel(own_v, total, new_v):
    own = own_v[...]
    new_v[...] = own - step_rate * (total[...] + ridge_weight * own)


def u_new_kernel(entries, own_u, *refs):
    parts, (new_u, loss_out) = refs[:-2], refs[-2:]
    own = own_u[...]
    rows = own.shape[0]
    total = parts[0][:rows, :].astype(f32)
    loss = read_loss(parts[0].at[rows:])
    for part in parts[1:]:
        total += part[:rows, :].astype(f32)
        loss += read_loss(part.at[rows:])
    new_u[...] = own - step_rate * (total + ridge_weight * own)
    loss_out[...] = (loss * (1.0 / entries))[0:1, 0:1]


def per_device(factor_u, factor_v, values, mask_words, tile_cols):
    slots, tile = values.shape[2], values.shape[-1]
    rank = factor_u.shape[-1]
    n_rows, n_cols = lax.axis_size("rows"), lax.axis_size("cols")
    block_rows, v_rows = factor_u.shape[1], factor_v.shape[1]
    far = far_order(n_cols)
    pairs = n_cols // 2

    def send_cols(x, bit):
        return lax.ppermute(x, "cols", partners(n_cols, bit))

    def send_rows(x, bit):
        return lax.ppermute(x, "rows", partners(n_rows, bit))

    own_u, own_v = factor_u[0], factor_v[0]
    u_low, v_low = own_u.astype(bf16), own_v.astype(bf16)
    tile_values, words, column_ids = values[0, 0], mask_words[0, 0], tile_cols[0, 0]
    tile_values, words, column_ids = call(
        fetch_kernel,
        tuple(sds(x.shape, x.dtype) for x in (tile_values, words, column_ids)),
        (tile_values, words, column_ids),
        [pltpu.SemaphoreType.DMA((3,))],
        {i: pltpu.HBM for i in range(3)},
    )

    v_blocks = {0: v_low}
    for q in row_order(n_rows):
        v_blocks[q] = send_rows(v_low, q)
    u_blocks = {0: u_low}
    for q in far:
        u_blocks[q] = send_cols(u_low, q)
    for q in [0] + far:
        u_blocks[q ^ 1] = send_cols(u_blocks[q], 1)

    share = sds((v_rows + LOSS_ROWS, rank), bf16)
    low, v_band, *v_parts = call(
        functools.partial(tile_kernel, n_cols, n_rows, tile),
        (sds((slots, tile, tile), bf16), sds((n_rows * v_rows, rank), bf16)) + (share,) * n_rows,
        (
            column_ids,
            tile_values,
            words,
            own_u,
            own_v,
            *[u_blocks[q] for q in range(n_cols)],
            *[v_blocks[q] for q in range(n_rows)],
        ),
        [pltpu.VMEM((n_rows * v_rows, rank), f32)],
        {0: pltpu.SMEM},
        4 * slots * tile * tile * rank,
    )
    v_got = [send_rows(v_parts[q], q) for q in row_order(n_rows)]
    part = sds((pairs, block_rows, rank), bf16)
    same, cross = call(
        functools.partial(rows_kernel, n_cols, tile),
        (part, part),
        (column_ids, low, v_band),
        (),
        {0: pltpu.SMEM},
        2 * slots * tile * tile * rank,
    )
    got = send_cols(cross, 1)
    v_total, loss = call(
        v_sum_kernel, (sds((v_rows, rank), f32), sds((8, rank), f32)), (v_parts[0], *v_got)
    )
    loss_other = send_cols(loss, 1)
    wide = sds((block_rows + LOSS_ROWS, rank), bf16)
    sums = call(carry_kernel, (wide,) * pairs, (loss, loss_other, same, got))
    u_got = [send_cols(sums[q // 2], q) for q in far]
    new_v = call(v_new_kernel, sds((v_rows, rank), f32), (own_v, v_total))
    entries = n_rows * n_cols * slots * tile * tile
    new_u, loss = call(
        functools.partial(u_new_kernel, entries),
        (sds((block_rows, rank), f32), sds((1, 1), f32)),
        (own_u, sums[0], *u_got),
    )
    return new_u[None], new_v[None], loss.reshape(())


def solution(mesh):
    in_specs = (
        P("rows", "cols", None),
        P("cols", "rows", None),
        P("rows", "cols", None, None, None),
        P("rows", "cols", None, None, None),
        P("rows", "cols", None),
    )
    out_specs = (P("rows", "cols", None), P("cols", "rows", None), P())
    return jax.shard_map(
        per_device, mesh=mesh, in_specs=in_specs, out_specs=out_specs, check_vma=False
    )
```

profile of v0, /device:TPU:0, one launch (start us, length us, event | category | flops | bytes accessed | tf_op | source)
XLA Modules:
  0.0 39.9 jit_solution(11425771616999128135)
XLA Ops:
  0.7 1.0 %bitcast_convert_fusion.1.refs_5_ = bf16[256,128]{1,0:T(8,128)(2,1)S(1)} fusion(f32[1,256,128]{2,1,0:T(8,128)} %param.5), kind=kLoop, calls=%fused_computation.1 | loop fusion | flops 32768 | bytes 196608 | tf_op jit(solution)/shard_map/convert_element_type | solution.py:189
  1.6 5.1 %collective-permute-start.5 = (bf16[256,128]{1,0:T(8,128)(2,1)S(1)}, bf16[256,128]{1,0:T(8,128)(2,1)S(1)}, u32[]{:S(2)}, u32[]{:S(2)}) collective-permute-start(bf16[256,128]{1,0:T(8,128)(2,1)S(1)} %bitcast_convert_fusion.1.refs_5_), channel_id=1, source_target_pairs={{0,6},{1,7},{2,4},{3,5},{4,2},{5,3},{6,0},{7,1},{8,14},{9,15},{10,... | collective-permute-start | bytes 196616 | tf_op jit(solution)/shard_map/ppermute | solution.py:183
  6.7 0.6 %collective-permute-start.1 = (bf16[256,128]{1,0:T(8,128)(2,1)S(1)}, bf16[256,128]{1,0:T(8,128)(2,1)S(1)}, u32[]{:S(2)}, u32[]{:S(2)}) collective-permute-start(bf16[256,128]{1,0:T(8,128)(2,1)S(1)} %bitcast_convert_fusion.1.refs_5_), channel_id=1, source_target_pairs={{0,2},{1,3},{2,0},{3,1},{4,6},{5,7},{6,4},{7,5},{8,10},{9,11},{10,... | collective-permute-start | bytes 196616 | tf_op jit(solution)/shard_map/ppermute | solution.py:183
  7.3 2.7 %collective-permute-start.9 = (bf16[128,128]{1,0:T(8,128)(2,1)S(1)}, bf16[128,128]{1,0:T(8,128)(2,1)S(1)}, u32[]{:S(2)}, u32[]{:S(2)}) collective-permute-start(bf16[128,128]{1,0:T(8,128)(2,1)S(1)} %bitcast_convert_fusion.refs_13_), channel_id=1, source_target_pairs={{0,24},{8,16},{16,8},{24,0},{1,25},{9,17},{17,9},{25,1},{2,26},{10... | collective-permute-start | bytes 98312 | tf_op jit(solution)/shard_map/ppermute | solution.py:186
  10.0 0.5 %collective-permute-start.8 = (bf16[128,128]{1,0:T(8,128)(2,1)S(1)}, bf16[128,128]{1,0:T(8,128)(2,1)S(1)}, u32[]{:S(2)}, u32[]{:S(2)}) collective-permute-start(bf16[128,128]{1,0:T(8,128)(2,1)S(1)} %bitcast_convert_fusion.refs_13_), channel_id=1, source_target_pairs={{0,16},{8,24},{16,0},{24,8},{1,17},{9,25},{17,1},{25,9},{2,18},{10... | collective-permute-start | bytes 98312 | tf_op jit(solution)/shard_map/ppermute | solution.py:186
  10.5 1.7 %collective-permute-done.9.refs_16_ = bf16[128,128]{1,0:T(8,128)(2,1)S(1)} collective-permute-done((bf16[128,128]{1,0:T(8,128)(2,1)S(1)}, bf16[128,128]{1,0:T(8,128)(2,1)S(1)}, u32[]{:S(2)}, u32[]{:S(2)}) %collective-permute-start.9) | collective-permute-done | bytes 32800 | tf_op jit(solution)/shard_map/ppermute | solution.py:186
  12.2 0.5 %collective-permute-start.6 = (bf16[256,128]{1,0:T(8,128)(2,1)S(1)}, bf16[256,128]{1,0:T(8,128)(2,1)S(1)}, u32[]{:S(2)}, u32[]{:S(2)}) collective-permute-start(bf16[256,128]{1,0:T(8,128)(2,1)S(1)} %collective-permute-done.5.refs_11_), channel_id=1, source_target_pairs={{0,1},{1,0},{2,3},{3,2},{4,5},{5,4},{6,7},{7,6},{8,9},{9,8},{10,11... | collective-permute-start | bytes 196616 | tf_op jit(solution)/shard_map/ppermute | solution.py:183
  12.8 0.4 %collective-permute-start.2 = (bf16[256,128]{1,0:T(8,128)(2,1)S(1)}, bf16[256,128]{1,0:T(8,128)(2,1)S(1)}, u32[]{:S(2)}, u32[]{:S(2)}) collective-permute-start(bf16[256,128]{1,0:T(8,128)(2,1)S(1)} %collective-permute-done.1.refs_7_), channel_id=1, source_target_pairs={{0,1},{1,0},{2,3},{3,2},{4,5},{5,4},{6,7},{7,6},{8,9},{9,8},{10,11... | collective-permute-start | bytes 196616 | tf_op jit(solution)/shard_map/ppermute | solution.py:183
  13.2 0.7 %collective-permute-done.8.refs_15_ = bf16[128,128]{1,0:T(8,128)(2,1)S(1)} collective-permute-done((bf16[128,128]{1,0:T(8,128)(2,1)S(1)}, bf16[128,128]{1,0:T(8,128)(2,1)S(1)}, u32[]{:S(2)}, u32[]{:S(2)}) %collective-permute-start.8) | collective-permute-done | bytes 32800 | tf_op jit(solution)/shard_map/ppermute | solution.py:186
  13.9 1.0 %collective-permute-start.7 = (bf16[128,128]{1,0:T(8,128)(2,1)S(1)}, bf16[128,128]{1,0:T(8,128)(2,1)S(1)}, u32[]{:S(2)}, u32[]{:S(2)}) collective-permute-start(bf16[128,128]{1,0:T(8,128)(2,1)S(1)} %bitcast_convert_fusion.refs_13_), channel_id=1, source_target_pairs={{0,8},{8,0},{16,24},{24,16},{1,9},{9,1},{17,25},{25,17},{2,10},{10... | collective-permute-start | bytes 98312 | tf_op jit(solution)/shard_map/ppermute | solution.py:186
  14.9 0.7 %copy-done.4 = s32[1,1,8]{2,1,0:T(1,128)S(1)} copy-done((s32[1,1,8]{2,1,0:T(1,128)S(1)}, s32[1,1,8]{2,1,0:T(1,128)}, u32[]{:S(2)}) %copy-start.4) | copy-done | bytes 56
  15.5 1.2 %copy-done.1 = bf16[1,1,8,256,256]{4,3,2,1,0:T(8,128)(2,1)S(1)} copy-done((bf16[1,1,8,256,256]{4,3,2,1,0:T(8,128)(2,1)S(1)}, bf16[1,1,8,256,256]{4,3,2,1,0:T(8,128)(2,1)}, u32[]{:S(2)}) %copy-start.1) | copy-done | bytes 1048600
  16.8 0.3 shard_map.76
  17.0 0.8 %collective-permute-done.7.refs_14_ = bf16[128,128]{1,0:T(8,128)(2,1)S(1)} collective-permute-done((bf16[128,128]{1,0:T(8,128)(2,1)S(1)}, bf16[128,128]{1,0:T(8,128)(2,1)S(1)}, u32[]{:S(2)}, u32[]{:S(2)}) %collective-permute-start.7) | collective-permute-done | bytes 32800 | tf_op jit(solution)/shard_map/ppermute | solution.py:186
  17.9 1.8 %shard_map.77 = (bf16[8,256,256]{2,1,0:T(8,128)(2,1)S(1)}, bf16[512,128]{1,0:T(8,128)(2,1)S(1)}, bf16[144,128]{1,0:T(8,128)(2,1)S(1)}, bf16[144,128]{1,0:T(8,128...) custom-call(s32[8]{0:T(128)S(1)} %get-tuple-element.22.refs_0_.column_ids, ...), custom_call_target="tpu_custom_call" | custom-call | flops 268435456 | tf_op jit(solution)/shard_map/pallas_call | solution.py:36
  19.6 1.0 %shard_map.79 = (bf16[4,256,128]{2,1,0:T(8,128)(2,1)S(1)}, bf16[4,256,128]{2,1,0:T(8,128)(2,1)S(1)}) custom-call(s32[8]{0:T(128)S(1)} %get-tuple-element.22.refs_0_.column_ids, bf16[8,256,256]{2,1,0:T(8,128)(2,1)S(1)} %get-tuple-element.30.low, bf16[512,128]{1,0:T(8,128)(2,1)S(1)} %get-tuple-element.31.v_band), custom_call_target="tpu_custom_call" | custom-call | flops 134217728 | tf_op jit(solution)/shard_map/pallas_call | solution.py:36
  20.7 1.0 %collective-permute-start.10 = (bf16[144,128]{1,0:T(8,128)(2,1)S(1)}, bf16[144,128]{1,0:T(8,128)(2,1)S(1)}, u32[]{:S(2)}, u32[]{:S(2)}) collective-permute-start(bf16[144,128]{1,0:T(8,128)(2,1)S(1)} %get-tuple-element.26), channel_id=1, source_target_pairs={{0,8},{8,0},{16,24},{24,16},{1,9},{9,1},{17,25},{25,17},{2,10},{10... | collective-permute-start | bytes 110600 | tf_op jit(solution)/shard_map/ppermute | solution.py:186
  21.7 1.5 %collective-permute-start.11 = (bf16[144,128]{1,0:T(8,128)(2,1)S(1)}, bf16[144,128]{1,0:T(8,128)(2,1)S(1)}, u32[]{:S(2)}, u32[]{:S(2)}) collective-permute-start(bf16[144,128]{1,0:T(8,128)(2,1)S(1)} %get-tuple-element.27), channel_id=1, source_target_pairs={{0,16},{8,24},{16,0},{24,8},{1,17},{9,25},{17,1},{25,9},{2,18},{10... | collective-permute-start | bytes 110600 | tf_op jit(solution)/shard_map/ppermute | solution.py:186
  23.2 1.0 %collective-permute-start.12 = (bf16[144,128]{1,0:T(8,128)(2,1)S(1)}, bf16[144,128]{1,0:T(8,128)(2,1)S(1)}, u32[]{:S(2)}, u32[]{:S(2)}) collective-permute-start(bf16[144,128]{1,0:T(8,128)(2,1)S(1)} %get-tuple-element.28), channel_id=1, source_target_pairs={{0,24},{8,16},{16,8},{24,0},{1,25},{9,17},{17,9},{25,1},{2,26},{10... | collective-permute-start | bytes 110600 | tf_op jit(solution)/shard_map/ppermute | solution.py:186
  24.2 0.5 %collective-permute-done.10.refs_1_ = bf16[144,128]{1,0:T(8,128)(2,1)S(1)} collective-permute-done((bf16[144,128]{1,0:T(8,128)(2,1)S(1)}, bf16[144,128]{1,0:T(8,128)(2,1)S(1)}, u32[]{:S(2)}, u32[]{:S(2)}) %collective-permute-start.10) | collective-permute-done | bytes 36896 | tf_op jit(solution)/shard_map/ppermute | solution.py:186
  24.7 1.0 %collective-permute-done.11.refs_2_ = bf16[144,128]{1,0:T(8,128)(2,1)S(1)} collective-permute-done((bf16[144,128]{1,0:T(8,128)(2,1)S(1)}, bf16[144,128]{1,0:T(8,128)(2,1)S(1)}, u32[]{:S(2)}, u32[]{:S(2)}) %collective-permute-start.11) | collective-permute-done | bytes 36896 | tf_op jit(solution)/shard_map/ppermute | solution.py:186
  25.7 2.4 %collective-permute-done.12.refs_3_ = bf16[144,128]{1,0:T(8,128)(2,1)S(1)} collective-permute-done((bf16[144,128]{1,0:T(8,128)(2,1)S(1)}, bf16[144,128]{1,0:T(8,128)(2,1)S(1)}, u32[]{:S(2)}, u32[]{:S(2)}) %collective-permute-start.12) | collective-permute-done | bytes 36896 | tf_op jit(solution)/shard_map/ppermute | solution.py:186
  28.2 1.2 %collective-permute-done.13.loss_other = f32[8,128]{1,0:T(8,128)S(1)} collective-permute-done((f32[8,128]{1,0:T(8,128)S(1)}, f32[8,128]{1,0:T(8,128)S(1)}, u32[]{:S(2)}, u32[]{:S(2)}) %collective-permute-start.13) | collective-permute-done | bytes 4128 | tf_op jit(solution)/shard_map/ppermute | solution.py:183
  29.4 0.1 shard_map.80
  29.4 2.2 %collective-permute-start.15 = (bf16[272,128]{1,0:T(8,128)(2,1)S(1)}, bf16[272,128]{1,0:T(8,128)(2,1)S(1)}, u32[]{:S(2)}, u32[]{:S(2)}) collective-permute-start(bf16[272,128]{1,0:T(8,128)(2,1)S(1)} %get-tuple-element.35), channel_id=1, source_target_pairs={{0,4},{1,5},{2,6},{3,7},{4,0},{5,1},{6,2},{7,3},{8,12},{9,13},{10,... | collective-permute-start | bytes 208904 | tf_op jit(solution)/shard_map/ppermute | solution.py:183
  31.7 1.5 %collective-permute-start.16 = (bf16[272,128]{1,0:T(8,128)(2,1)S(1)}, bf16[272,128]{1,0:T(8,128)(2,1)S(1)}, u32[]{:S(2)}, u32[]{:S(2)}) collective-permute-start(bf16[272,128]{1,0:T(8,128)(2,1)S(1)} %get-tuple-element.36), channel_id=1, source_target_pairs={{0,6},{1,7},{2,4},{3,5},{4,2},{5,3},{6,0},{7,1},{8,14},{9,15},{10,... | collective-permute-start | bytes 208904 | tf_op jit(solution)/shard_map/ppermute | solution.py:183
  33.2 0.5 %collective-permute-start.17 = (bf16[272,128]{1,0:T(8,128)(2,1)S(1)}, bf16[272,128]{1,0:T(8,128)(2,1)S(1)}, u32[]{:S(2)}, u32[]{:S(2)}) collective-permute-start(bf16[272,128]{1,0:T(8,128)(2,1)S(1)} %get-tuple-element.37), channel_id=1, source_target_pairs={{0,2},{1,3},{2,0},{3,1},{4,6},{5,7},{6,4},{7,5},{8,10},{9,11},{10,... | collective-permute-start | bytes 208904 | tf_op jit(solution)/shard_map/ppermute | solution.py:183
  33.7 0.6 %shard_map.82 = f32[128,128]{1,0:T(8,128)} custom-call(f32[128,128]{1,0:T(8,128)S(1)} %bitcast.14, f32[128,128]{1,0:T(8,128)S(1)} %get-tuple-element.39.total), custom_call_target="tpu_custom_call" | custom-call | tf_op jit(solution)/shard_map/pallas_call | solution.py:36
  34.3 3.5 %collective-permute-done.15.refs_1_ = bf16[272,128]{1,0:T(8,128)(2,1)S(1)} collective-permute-done((bf16[272,128]{1,0:T(8,128)(2,1)S(1)}, bf16[272,128]{1,0:T(8,128)(2,1)S(1)}, u32[]{:S(2)}, u32[]{:S(2)}) %collective-permute-start.15) | collective-permute-done | bytes 69664 | tf_op jit(solution)/shard_map/ppermute | solution.py:183
  37.9 0.4 %collective-permute-done.16.refs_2_ = bf16[272,128]{1,0:T(8,128)(2,1)S(1)} collective-permute-done((bf16[272,128]{1,0:T(8,128)(2,1)S(1)}, bf16[272,128]{1,0:T(8,128)(2,1)S(1)}, u32[]{:S(2)}, u32[]{:S(2)}) %collective-permute-start.16) | collective-permute-done | bytes 69664 | tf_op jit(solution)/shard_map/ppermute | solution.py:183
  38.3 0.9 %collective-permute-done.17.refs_3_ = bf16[272,128]{1,0:T(8,128)(2,1)S(1)} collective-permute-done((bf16[272,128]{1,0:T(8,128)(2,1)S(1)}, bf16[272,128]{1,0:T(8,128)(2,1)S(1)}, u32[]{:S(2)}, u32[]{:S(2)}) %collective-permute-start.17) | collective-permute-done | bytes 69664 | tf_op jit(solution)/shard_map/ppermute | solution.py:183
  39.1 0.7 %shard_map.81 = (f32[256,128]{1,0:T(8,128)}, f32[1,1]{1,0:T(1,128)}) custom-call(f32[256,128]{1,0:T(8,128)S(1)} %bitcast.11, bf16[272,128]{1,0:T(8,128)(2,1)S(1)} %get-tuple-element.34.refs_0_, bf16[272,128]{1,0:T(8,128)(2,1)S(1)} %collective-permute-done.15.refs_1_, bf16[272,128]{1,0:T(8,128)(2,1)S(1)} %collective-permute-done.16.refs_2_, ...), custom_call_target="tpu_custom_call" | custom-call | tf_op jit(solution)/shard_map/pallas_call | solution.py:36
  (23 shorter events, 0.3 us)
Async XLA Ops:
  0.6 6.7 %copy-start.2 = (f32[1,128,128]{2,1,0:T(8,128)S(1)}, f32[1,128,128]{2,1,0:T(8,128)}, u32[]{:S(2)}) copy-start(f32[1,128,128]{2,1,0:T(8,128)} %param.6) | copy-start | bytes 196612
  0.6 14.3 %copy-start.3 = (s32[1,1,8,16,256]{4,3,2,1,0:T(8,128)S(1)}, s32[1,1,8,16,256]{4,3,2,1,0:T(8,128)}, u32[]{:S(2)}) copy-start(s32[1,1,8,16,256]{4,3,2,1,0:T(8,128)} %param.8) | copy-start | bytes 393220
  1.6 10.6 %collective-permute-start.5 = (bf16[256,128]{1,0:T(8,128)(2,1)S(1)}, bf16[256,128]{1,0:T(8,128)(2,1)S(1)}, u32[]{:S(2)}, u32[]{:S(2)}) collective-permute-start(bf16[256,128]{1,0:T(8,128)(2,1)S(1)} %bitcast_convert_fusion.1.refs_5_), channel_id=1, source_target_pairs={{0,6},{1,7},{2,4},{3,5},{4,2},{5,3},{6,0},{7,1},{8,14},{9,15},{10,... | collective-permute-start | bytes 196616 | tf_op jit(solution)/shard_map/ppermute | solution.py:183
  6.7 6.0 %collective-permute-start.3 = (bf16[256,128]{1,0:T(8,128)(2,1)S(1)}, bf16[256,128]{1,0:T(8,128)(2,1)S(1)}, u32[]{:S(2)}, u32[]{:S(2)}) collective-permute-start(bf16[256,128]{1,0:T(8,128)(2,1)S(1)} %bitcast_convert_fusion.1.refs_5_), channel_id=1, source_target_pairs={{0,4},{1,5},{2,6},{3,7},{4,0},{5,1},{6,2},{7,3},{8,12},{9,13},{10,... | collective-permute-start | bytes 196616 | tf_op jit(solution)/shard_map/ppermute | solution.py:183
  6.7 6.1 %collective-permute-start.1 = (bf16[256,128]{1,0:T(8,128)(2,1)S(1)}, bf16[256,128]{1,0:T(8,128)(2,1)S(1)}, u32[]{:S(2)}, u32[]{:S(2)}) collective-permute-start(bf16[256,128]{1,0:T(8,128)(2,1)S(1)} %bitcast_convert_fusion.1.refs_5_), channel_id=1, source_target_pairs={{0,2},{1,3},{2,0},{3,1},{4,6},{5,7},{6,4},{7,5},{8,10},{9,11},{10,... | collective-permute-start | bytes 196616 | tf_op jit(solution)/shard_map/ppermute | solution.py:183
  7.3 4.9 %collective-permute-start.9 = (bf16[128,128]{1,0:T(8,128)(2,1)S(1)}, bf16[128,128]{1,0:T(8,128)(2,1)S(1)}, u32[]{:S(2)}, u32[]{:S(2)}) collective-permute-start(bf16[128,128]{1,0:T(8,128)(2,1)S(1)} %bitcast_convert_fusion.refs_13_), channel_id=1, source_target_pairs={{0,24},{8,16},{16,8},{24,0},{1,25},{9,17},{17,9},{25,1},{2,26},{10... | collective-permute-start | bytes 98312 | tf_op jit(solution)/shard_map/ppermute | solution.py:186
  10.0 3.9 %collective-permute-start.8 = (bf16[128,128]{1,0:T(8,128)(2,1)S(1)}, bf16[128,128]{1,0:T(8,128)(2,1)S(1)}, u32[]{:S(2)}, u32[]{:S(2)}) collective-permute-start(bf16[128,128]{1,0:T(8,128)(2,1)S(1)} %bitcast_convert_fusion.refs_13_), channel_id=1, source_target_pairs={{0,16},{8,24},{16,0},{24,8},{1,17},{9,25},{17,1},{25,9},{2,18},{10... | collective-permute-start | bytes 98312 | tf_op jit(solution)/shard_map/ppermute | solution.py:186
  12.2 5.6 %collective-permute-start = (bf16[256,128]{1,0:T(8,128)(2,1)S(1)}, bf16[256,128]{1,0:T(8,128)(2,1)S(1)}, u32[]{:S(2)}, u32[]{:S(2)}) collective-permute-start(bf16[256,128]{1,0:T(8,128)(2,1)S(1)} %bitcast_convert_fusion.1.refs_5_), channel_id=1, source_target_pairs={{0,1},{1,0},{2,3},{3,2},{4,5},{5,4},{6,7},{7,6},{8,9},{9,8},{10,11... | collective-permute-start | bytes 196616 | tf_op jit(solution)/shard_map/ppermute | solution.py:183
  12.2 5.6 %collective-permute-start.6 = (bf16[256,128]{1,0:T(8,128)(2,1)S(1)}, bf16[256,128]{1,0:T(8,128)(2,1)S(1)}, u32[]{:S(2)}, u32[]{:S(2)}) collective-permute-start(bf16[256,128]{1,0:T(8,128)(2,1)S(1)} %collective-permute-done.5.refs_11_), channel_id=1, source_target_pairs={{0,1},{1,0},{2,3},{3,2},{4,5},{5,4},{6,7},{7,6},{8,9},{9,8},{10,11... | collective-permute-start | bytes 196616 | tf_op jit(solution)/shard_map/ppermute | solution.py:183
  12.7 5.1 %collective-permute-start.4 = (bf16[256,128]{1,0:T(8,128)(2,1)S(1)}, bf16[256,128]{1,0:T(8,128)(2,1)S(1)}, u32[]{:S(2)}, u32[]{:S(2)}) collective-permute-start(bf16[256,128]{1,0:T(8,128)(2,1)S(1)} %collective-permute-done.3.refs_9_), channel_id=1, source_target_pairs={{0,1},{1,0},{2,3},{3,2},{4,5},{5,4},{6,7},{7,6},{8,9},{9,8},{10,11... | collective-permute-start | bytes 196616 | tf_op jit(solution)/shard_map/ppermute | solution.py:183
  12.8 5.0 %collective-permute-start.2 = (bf16[256,128]{1,0:T(8,128)(2,1)S(1)}, bf16[256,128]{1,0:T(8,128)(2,1)S(1)}, u32[]{:S(2)}, u32[]{:S(2)}) collective-permute-start(bf16[256,128]{1,0:T(8,128)(2,1)S(1)} %collective-permute-done.1.refs_7_), channel_id=1, source_target_pairs={{0,1},{1,0},{2,3},{3,2},{4,5},{5,4},{6,7},{7,6},{8,9},{9,8},{10,11... | collective-permute-start | bytes 196616 | tf_op jit(solution)/shard_map/ppermute | solution.py:183
  13.9 3.9 %collective-permute-start.7 = (bf16[128,128]{1,0:T(8,128)(2,1)S(1)}, bf16[128,128]{1,0:T(8,128)(2,1)S(1)}, u32[]{:S(2)}, u32[]{:S(2)}) collective-permute-start(bf16[128,128]{1,0:T(8,128)(2,1)S(1)} %bitcast_convert_fusion.refs_13_), channel_id=1, source_target_pairs={{0,8},{8,0},{16,24},{24,16},{1,9},{9,1},{17,25},{25,17},{2,10},{10... | collective-permute-start | bytes 98312 | tf_op jit(solution)/shard_map/ppermute | solution.py:186
  14.9 0.7 %copy-start.4 = (s32[1,1,8]{2,1,0:T(1,128)S(1)}, s32[1,1,8]{2,1,0:T(1,128)}, u32[]{:S(2)}) copy-start(s32[1,1,8]{2,1,0:T(1,128)} %param.9) | copy-start | bytes 100
  15.5 1.2 %copy-start.1 = (bf16[1,1,8,256,256]{4,3,2,1,0:T(8,128)(2,1)S(1)}, bf16[1,1,8,256,256]{4,3,2,1,0:T(8,128)(2,1)}, u32[]{:S(2)}) copy-start(bf16[1,1,8,256,256]{4,3,2,1,0:T(8,128)(2,1)} %param.7) | copy-start | bytes 3145732
  16.8 1.1 %copy-start = (f32[1,256,128]{2,1,0:T(8,128)S(1)}, f32[1,256,128]{2,1,0:T(8,128)}, u32[]{:S(2)}) copy-start(f32[1,256,128]{2,1,0:T(8,128)} %param.5) | copy-start | bytes 393220
  20.6 8.8 %collective-permute-start.14 = (bf16[4,256,128]{2,1,0:T(8,128)(2,1)S(1)}, bf16[4,256,128]{2,1,0:T(8,128)(2,1)S(1)}, u32[]{:S(2)}, u32[]{:S(2)}) collective-permute-start(bf16[4,256,128]{2,1,0:T(8,128)(2,1)S(1)} %get-tuple-element.33), channel_id=1, source_target_pairs={{0,1},{1,0},{2,3},{3,2},{4,5},{5,4},{6,7},{7,6},{8,9},{9,8},{10,11... | collective-permute-start | bytes 786440 | tf_op jit(solution)/shard_map/ppermute | solution.py:183
  20.7 4.0 %collective-permute-start.10 = (bf16[144,128]{1,0:T(8,128)(2,1)S(1)}, bf16[144,128]{1,0:T(8,128)(2,1)S(1)}, u32[]{:S(2)}, u32[]{:S(2)}) collective-permute-start(bf16[144,128]{1,0:T(8,128)(2,1)S(1)} %get-tuple-element.26), channel_id=1, source_target_pairs={{0,8},{8,0},{16,24},{24,16},{1,9},{9,1},{17,25},{25,17},{2,10},{10... | collective-permute-start | bytes 110600 | tf_op jit(solution)/shard_map/ppermute | solution.py:186
  21.7 4.0 %collective-permute-start.11 = (bf16[144,128]{1,0:T(8,128)(2,1)S(1)}, bf16[144,128]{1,0:T(8,128)(2,1)S(1)}, u32[]{:S(2)}, u32[]{:S(2)}) collective-permute-start(bf16[144,128]{1,0:T(8,128)(2,1)S(1)} %get-tuple-element.27), channel_id=1, source_target_pairs={{0,16},{8,24},{16,0},{24,8},{1,17},{9,25},{17,1},{25,9},{2,18},{10... | collective-permute-start | bytes 110600 | tf_op jit(solution)/shard_map/ppermute | solution.py:186
  23.2 4.9 %collective-permute-start.12 = (bf16[144,128]{1,0:T(8,128)(2,1)S(1)}, bf16[144,128]{1,0:T(8,128)(2,1)S(1)}, u32[]{:S(2)}, u32[]{:S(2)}) collective-permute-start(bf16[144,128]{1,0:T(8,128)(2,1)S(1)} %get-tuple-element.28), channel_id=1, source_target_pairs={{0,24},{8,16},{16,8},{24,0},{1,25},{9,17},{17,9},{25,1},{2,26},{10... | collective-permute-start | bytes 110600 | tf_op jit(solution)/shard_map/ppermute | solution.py:186
  28.1 1.2 %collective-permute-start.13 = (f32[8,128]{1,0:T(8,128)S(1)}, f32[8,128]{1,0:T(8,128)S(1)}, u32[]{:S(2)}, u32[]{:S(2)}) collective-permute-start(f32[8,128]{1,0:T(8,128)S(1)} %get-tuple-element.29.loss), channel_id=1, source_target_pairs={{0,1},{1,0},{2,3},{3,2},{4,5},{5,4},{6,7},{7,6},{8,9},{9,8},{10,11... | collective-permute-start | bytes 12296 | tf_op jit(solution)/shard_map/ppermute | solution.py:183
  29.4 8.4 %collective-permute-start.15 = (bf16[272,128]{1,0:T(8,128)(2,1)S(1)}, bf16[272,128]{1,0:T(8,128)(2,1)S(1)}, u32[]{:S(2)}, u32[]{:S(2)}) collective-permute-start(bf16[272,128]{1,0:T(8,128)(2,1)S(1)} %get-tuple-element.35), channel_id=1, source_target_pairs={{0,4},{1,5},{2,6},{3,7},{4,0},{5,1},{6,2},{7,3},{8,12},{9,13},{10,... | collective-permute-start | bytes 208904 | tf_op jit(solution)/shard_map/ppermute | solution.py:183
  31.7 6.6 %collective-permute-start.16 = (bf16[272,128]{1,0:T(8,128)(2,1)S(1)}, bf16[272,128]{1,0:T(8,128)(2,1)S(1)}, u32[]{:S(2)}, u32[]{:S(2)}) collective-permute-start(bf16[272,128]{1,0:T(8,128)(2,1)S(1)} %get-tuple-element.36), channel_id=1, source_target_pairs={{0,6},{1,7},{2,4},{3,5},{4,2},{5,3},{6,0},{7,1},{8,14},{9,15},{10,... | collective-permute-start | bytes 208904 | tf_op jit(solution)/shard_map/ppermute | solution.py:183
  33.2 6.0 %collective-permute-start.17 = (bf16[272,128]{1,0:T(8,128)(2,1)S(1)}, bf16[272,128]{1,0:T(8,128)(2,1)S(1)}, u32[]{:S(2)}, u32[]{:S(2)}) collective-permute-start(bf16[272,128]{1,0:T(8,128)(2,1)S(1)} %get-tuple-element.37), channel_id=1, source_target_pairs={{0,2},{1,3},{2,0},{3,1},{4,6},{5,7},{6,4},{7,5},{8,10},{9,11},{10,... | collective-permute-start | bytes 208904 | tf_op jit(solution)/shard_map/ppermute | solution.py:183
where the time goes:
time: 40 us; the launch traced here: 39.9 us
  starting transfers between devices  18.8 us (47%)
  waiting for transfers between devices  13 us (32%)
  Pallas kernels  4.46 us (11%)
  local copies, waits for them, and re-layouts  1.89 us (5%)
  other arithmetic  0.96 us (2%)
  between operations  0.73 us (2%)
    ppermute x12, starting transfers between devices, send_cols(): return lax.ppermute(x, 'cols', partners(n_cols, bit))  11.1 us
    ppermute x6, starting transfers between devices, send_rows(): return lax.ppermute(x, 'rows', partners(n_rows, bit))  7.7 us
    ppermute x6, waiting for transfers between devices, send_rows(): return lax.ppermute(x, 'rows', partners(n_rows, bit))  7.02 us
    ppermute x12, waiting for transfers between devices, send_cols(): return lax.ppermute(x, 'cols', partners(n_cols, bit))  5.99 us
    pallas_call x7, Pallas kernels, call(): pl.pallas_call(body, out_shape=out_shape, in_specs=specs, out_specs=jax.t...  4.46 us
    unnamed x10, local copies, waits for them, and re-layouts  1.89 us
    convert_element_type x2, other arithmetic, per_device(): u_low, v_low = (own_u.astype(bf16), own_v.astype(bf16))  0.96 us
  transfers between devices with their start and end apart: 18, of which 10 were waited for; matrix products, arithmetic and copies ran while one was open for 0% of the time, Pallas kernels for 2%

commit v1 on v0

v1 whole, which is shorter than its diff:
```python
import functools

import jax
import jax.numpy as jnp
from jax import lax
from jax.experimental import pallas as pl
from jax.experimental.pallas import tpu as pltpu
from jax.sharding import PartitionSpec as P


step_rate = 0.01
ridge_weight = 0.1
bf16 = jnp.bfloat16
f32 = jnp.float32
LOSS_ROWS = 16
WORD_BITS = 16
PLAIN = 1
CROSS = 0
VMEM_LIMIT = 24 * 2**20
sds = jax.ShapeDtypeStruct


def partners(size, bit):
    return [(i, i ^ bit) for i in range(size)]


def bits_of(size):
    return [1 << i for i in range(size.bit_length() - 1)]


def far_order(n_cols):
    return [q ^ CROSS for q in sorted(range(2, n_cols, 2), key=lambda q: (q != 4, -q))]


def call(body, out_shape, args, scratch=(), spaces=None, flops=0):
    spaces = spaces or {}
    specs = [pl.BlockSpec(memory_space=spaces.get(i, pltpu.VMEM)) for i in range(len(args))]
    return pl.pallas_call(
        body,
        out_shape=out_shape,
        in_specs=specs,
        out_specs=jax.tree.map(lambda _: pl.BlockSpec(memory_space=pltpu.VMEM), out_shape),
        scratch_shapes=list(scratch),
        compiler_params=pltpu.CompilerParams(vmem_limit_bytes=VMEM_LIMIT),
        cost_estimate=pl.CostEstimate(flops=flops, bytes_accessed=0, transcendentals=0),
    )(*args)


def pack_loss(loss_row):
    width = loss_row.shape[-1]
    hi = loss_row.astype(bf16).astype(f32)
    mid = (loss_row - hi).astype(bf16).astype(f32)
    lo = loss_row - hi - mid
    which = lax.broadcasted_iota(jnp.int32, (LOSS_ROWS, width), 0)
    rows = jnp.where(which == 0, hi, jnp.where(which == 1, mid, jnp.where(which == 2, lo, 0.0)))
    return rows.astype(bf16)


def read_loss(block):
    rows = block[...].astype(f32)
    return rows[0:1] + rows[1:2] + rows[2:3]


def fetch_kernel(*refs):
    count = len(refs) // 2
    sems = refs[-1]
    copies = [
        pltpu.make_async_copy(refs[i], refs[count + i], sems.at[i]) for i in range(count)
    ]
    for copy in copies:
        copy.start()
    for copy in copies:
        copy.wait()


def stack_kernel(left, right, out):
    rows = left.shape[0]
    out[:rows, :] = left[...]
    out[rows:, :] = right[...]


def column_of(column_ids, slot):
    places = lax.broadcasted_iota(jnp.int32, column_ids.shape, 1)
    picked = jnp.where(places == slot, column_ids[...].astype(f32), 0.0)
    return jnp.sum(picked).astype(jnp.int32)


def tile_slots(places, tile, column_ids, values, words, u_blocks, v_band, low_out, right_out, v_total):
    col = lax.axis_index("cols")
    bit = jnp.left_shift(1, lax.broadcasted_iota(jnp.int32, (WORD_BITS, tile), 0))
    squares = jnp.zeros((8, tile), f32)
    tiles = u_blocks[0].shape[0] // tile
    for k, q in enumerate(places):
        for t in range(tiles):
            slot = (col ^ q) * tiles + t
            start = column_of(column_ids, slot) * tile
            left = u_blocks[k][t * tile : (t + 1) * tile, :]
            right = v_band[pl.ds(start, tile), :]
            predicted = lax.dot_general(
                left, right, (((1,), (1,)), ((), ())), preferred_element_type=f32
            )
            diff = predicted - values[slot].astype(f32)
            parts = []
            for w in range(tile // WORD_BITS):
                marks = jnp.broadcast_to(words[slot, w : w + 1, :], (WORD_BITS, tile))
                seen = jnp.bitwise_and(marks, bit) != 0
                parts.append(jnp.where(seen, diff[w * WORD_BITS : (w + 1) * WORD_BITS, :], 0.0))
            residual = jnp.concatenate(parts, axis=0)
            squares += jnp.sum((residual * residual).reshape(-1, 8, tile), axis=0)
            low = residual.astype(bf16)
            low_out[k * tiles + t] = low
            right_out[k * tiles + t] = right
            v_total[pl.ds(start, tile), :] += lax.dot_general(
                low, left, (((0,), (0,)), ((), ())), preferred_element_type=f32
            )
    return squares


def even_kernel(places, order_v, tile, *refs):
    column_ids, values, words = refs[:3]
    u_blocks, (v_stack, v_other, low_out, right_out, v_band, v_total, squares) = (
        refs[3:-7],
        refs[-7:],
    )
    row = lax.axis_index("rows")
    n_rows = len(order_v)
    v_rows = v_band.shape[0] // n_rows
    half = n_rows // 2
    for k, q in enumerate(order_v):
        source = v_stack if k < half else v_other
        v_band[pl.ds((row ^ q) * v_rows, v_rows), :] = source[
            (k % half) * v_rows : (k % half + 1) * v_rows, :
        ]
    v_total[...] = jnp.zeros_like(v_total)
    squares[...] = tile_slots(
        places, tile, column_ids, values, words, u_blocks, v_band, low_out, right_out, v_total
    )


def odd_kernel(places, n_rows, tile, *refs):
    column_ids, values, words, own_u, own_v, v_band, v_start, squares = refs[:8]
    u_blocks, (low_out, right_out, keep, send, loss_out, v_total) = refs[8:-6], refs[-6:]
    row = lax.axis_index("rows")
    v_total[...] = v_start[...]
    total = squares[...] + tile_slots(
        places, tile, column_ids, values, words, u_blocks, v_band, low_out, right_out, v_total
    )
    u_own = own_u[...]
    v_own = own_v[...]
    loss = 0.5 * jnp.sum(total) + 0.5 * ridge_weight * (
        jnp.sum(u_own * u_own) + jnp.sum(v_own * v_own)
    )
    loss_out[...] = jnp.full(loss_out.shape, loss, f32)
    v_rows = own_v.shape[0]
    keep[...] = v_total[pl.ds(row * v_rows, v_rows), :]
    for q in range(1, n_rows):
        send[q - 1] = v_total[pl.ds((row ^ q) * v_rows, v_rows), :].astype(bf16)


def rows_kernel(low_even, low_odd, right_even, right_odd, same, cross):
    pairs, tile = same.shape[0], low_even.shape[1]
    tiles = low_even.shape[0] // pairs
    for low, right, target in ((low_odd, right_odd, cross), (low_even, right_even, same)):
        for k in range(pairs):
            for t in range(tiles):
                slot = k * tiles + t
                grad = jnp.dot(low[slot], right[slot], preferred_element_type=f32)
                target[k, t * tile : (t + 1) * tile, :] = grad.astype(bf16)


def pack_kernel(loss, loss_other, blocks, *outs):
    total = loss[...] + loss_other[...]
    packed = pack_loss(total[0:1])
    rows = blocks.shape[1]
    for q, out in enumerate(outs[:-1]):
        out[:rows, :] = blocks[q]
        out[rows:, :] = packed
    outs[-1][...] = total


def carry_kernel(count, loss, *refs):
    blocks, outs = refs[:count], refs[count:]
    packed = pack_loss(loss[0:1])
    for block, out in zip(blocks, outs):
        rows = block.shape[0]
        out[:rows, :] = block[...]
        out[rows:, :] = packed


def pair_kernel(same, got, *outs):
    for q, out in enumerate(outs):
        out[...] = (same[q].astype(f32) + got[q].astype(f32)).astype(bf16)


def fold_kernel(keep, loss, *refs):
    parts, (total_out, loss_out) = refs[:-2], refs[-2:]
    rows = keep.shape[0]
    total, loss_sum = keep[...], loss[...]
    for part in parts:
        total += part[:rows, :].astype(f32)
        loss_sum += read_loss(part.at[rows:])
    total_out[...] = total
    loss_out[...] = loss_sum


def v_new_kernel(own_v, total, new_v):
    own = own_v[...]
    new_v[...] = own - step_rate * (total[...] + ridge_weight * own)


def u_new_kernel(entries, n_tiny, own_u, loss, *refs):
    tiny, parts, (new_u, loss_out) = refs[:n_tiny], refs[n_tiny:-2], refs[-2:]
    own = own_u[...]
    rows = own.shape[0]
    total = parts[0][:rows, :].astype(f32)
    for part in parts[1:]:
        total += part[:rows, :].astype(f32)
    loss_sum = loss[0:1]
    for part in parts[1 + n_tiny :]:
        loss_sum += read_loss(part.at[rows:])
    for other in tiny:
        loss_sum += other[0:1]
    new_u[...] = own - step_rate * (total + ridge_weight * own)
    loss_out[...] = (loss_sum * (1.0 / entries))[0:1, 0:1]


def per_device(factor_u, factor_v, values, mask_words, tile_cols):
    slots, tile = values.shape[2], values.shape[-1]
    rank = factor_u.shape[-1]
    n_rows, n_cols = lax.axis_size("rows"), lax.axis_size("cols")
    block_rows, v_rows = factor_u.shape[1], factor_v.shape[1]
    far = far_order(n_cols)
    direct = [0] + far
    swapped = [q ^ 1 for q in direct]
    pairs = n_cols // 2
    row_bits = bits_of(n_rows)

    def send_cols(x, bit):
        return lax.ppermute(x, "cols", partners(n_cols, bit))

    def send_rows(x, bit):
        return lax.ppermute(x, "rows", partners(n_rows, bit))

    own_u, own_v = factor_u[0], factor_v[0]
    u_low, v_low = own_u.astype(bf16), own_v.astype(bf16)
    held = (values[0, 0], mask_words[0, 0], tile_cols[0, 0])
    tile_values, words, column_ids = call(
        fetch_kernel,
        tuple(sds(x.shape, x.dtype) for x in held),
        tuple(pltpu.with_memory_space_constraint(x, pltpu.HBM) for x in held),
        [pltpu.SemaphoreType.DMA((len(held),))],
        {i: pltpu.HBM for i in range(len(held))},
    )
    column_ids = column_ids.reshape(1, slots)

    v_stack, order_v = v_low, [0]
    for b in row_bits:
        v_other = send_rows(v_stack, b)
        order_v = order_v + [q ^ b for q in order_v]
        if b != row_bits[-1]:
            shape = sds((2 * v_stack.shape[0], rank), bf16)
            v_stack = call(stack_kernel, shape, (v_stack, v_other))
    u_blocks = {0: u_low}
    for q in far:
        u_blocks[q] = send_cols(u_low, q)
    for q in direct:
        u_blocks[q ^ 1] = send_cols(u_blocks[q], 1)

    low_shape = sds((slots // 2, tile, tile), bf16)
    right_shape = sds((slots // 2, tile, rank), bf16)
    band = (n_rows * v_rows, rank)
    tile_flops = 2 * slots * tile * tile * rank
    low_even, right_even, v_band, v_start, squares = call(
        functools.partial(even_kernel, direct, order_v, tile),
        (low_shape, right_shape, sds(band, bf16), sds(band, f32), sds((8, tile), f32)),
        (
            column_ids,
            tile_values,
            words,
            *[u_blocks[q] for q in direct],
            v_stack,
            v_other,
        ),
        flops=tile_flops,
    )
    low_odd, right_odd, keep, send, loss = call(
        functools.partial(odd_kernel, swapped, n_rows, tile),
        (
            low_shape,
            right_shape,
            sds((v_rows, rank), f32),
            sds((n_rows - 1, v_rows, rank), bf16),
            sds((8, rank), f32),
        ),
        (
            column_ids,
            tile_values,
            words,
            own_u,
            own_v,
            v_band,
            v_start,
            squares,
            *[u_blocks[q] for q in swapped],
        ),
        [pltpu.VMEM(band, f32)],
        flops=tile_flops,
    )
    loss_other = send_cols(loss, 1)
    part = sds((pairs, block_rows, rank), bf16)
    same, cross = call(
        rows_kernel, (part, part), (low_even, low_odd, right_even, right_odd), flops=tile_flops
    )
    got = send_cols(cross, 1)
    loss_shape = sds((8, rank), f32)
    share = sds((v_rows + LOSS_ROWS, rank), bf16)
    *shares, loss = call(
        pack_kernel, (share,) * (n_rows - 1) + (loss_shape,), (loss, loss_other, send)
    )
    block = sds((block_rows, rank), bf16)
    sums = call(pair_kernel, (block,) * pairs, (same, got))
    plain, carrying = far[:PLAIN], far[PLAIN:]
    u_got = [send_cols(sums[direct.index(q)], q) for q in plain]
    v_got = [send_rows(x, q) for q, x in enumerate(shares, 1)]
    keep, loss = call(fold_kernel, (sds((v_rows, rank), f32), loss_shape), (keep, loss, *v_got))
    wide = sds((block_rows + LOSS_ROWS, rank), bf16)
    carried = call(
        functools.partial(carry_kernel, len(carrying)),
        (wide,) * len(carrying),
        (loss, *[sums[direct.index(q)] for q in carrying]),
    )
    u_got += [send_cols(x, q) for q, x in zip(carrying, carried)]
    tiny = [send_cols(loss, q) for q in plain]
    new_v = call(v_new_kernel, sds((v_rows, rank), f32), (own_v, keep))
    entries = n_rows * n_cols * slots * tile * tile
    new_u, loss = call(
        functools.partial(u_new_kernel, entries, len(tiny)),
        (sds((block_rows, rank), f32), sds((1, 1), f32)),
        (own_u, loss, *tiny, sums[0], *u_got),
    )
    return new_u[None], new_v[None], loss.reshape(())


def solution(mesh):
    in_specs = (
        P("rows", "cols", None),
        P("cols", "rows", None),
        P("rows", "cols", None, None, None),
        P("rows", "cols", None, None, None),
        P("rows", "cols", None),
    )
    out_specs = (P("rows", "cols", None), P("cols", "rows", None), P())
    return jax.shard_map(
        per_device, mesh=mesh, in_specs=in_specs, out_specs=out_specs, check_vma=False
    )
```

time: 40 us -> 38 us (0.950)
  waiting for transfers between devices: 13 us -> 10.9 us
  local copies, waits for them, and re-layouts: 1.89 us -> 0.01 us
  starting transfers between devices: 18.8 us -> 20 us
  Pallas kernels: 4.46 us -> 5.2 us
    ppermute x12 -> x13, waiting for transfers between devices: 5.99 us -> 3.64 us  [send_cols(): return lax.ppermute(x, 'cols', partners(n_cols, bit))]
    ppermute x12 -> x13, starting transfers between devices: 11.1 us -> 13.4 us  [send_cols(): return lax.ppermute(x, 'cols', partners(n_cols, bit))]
    unnamed x10 -> x4, local copies, waits for them, and re-layouts: 1.89 us -> 0.01 us
    ppermute x6 -> x5, starting transfers between devices: 7.7 us -> 6.63 us  [send_rows(): return lax.ppermute(x, 'rows', partners(n_rows, bit))]
    pallas_call x7 -> x11, Pallas kernels: 4.46 us -> 5.2 us  [call(): pl.pallas_call(body, out_shape=out_shape, in_specs=specs, out_specs=jax.t...]
    ppermute x6 -> x5, waiting for transfers between devices: 7.02 us -> 7.25 us  [send_rows(): return lax.ppermute(x, 'rows', partners(n_rows, bit))]
  transfers between devices with their start and end apart: 18 -> 18, of which waited for: 10 -> 8; matrix products, arithmetic and copies ran while one was open for 0% -> 0% of each run, Pallas kernels for 2% -> 8%
where the time goes in v1:
time: 38 us; the launch traced here: 37.8 us
  starting transfers between devices  20 us (53%)
  waiting for transfers between devices  10.9 us (29%)
  Pallas kernels  5.2 us (14%)
  other arithmetic  0.95 us (2%)
  between operations  0.76 us (2%)
    ppermute x13, starting transfers between devices, send_cols(): return lax.ppermute(x, 'cols', partners(n_cols, bit))  13.4 us
    ppermute x5, waiting for transfers between devices, send_rows(): return lax.ppermute(x, 'rows', partners(n_rows, bit))  7.25 us
    ppermute x5, starting transfers between devices, send_rows(): return lax.ppermute(x, 'rows', partners(n_rows, bit))  6.63 us
    pallas_call x11, Pallas kernels, call(): pl.pallas_call(body, out_shape=out_shape, in_specs=specs, out_specs=jax.t...  5.2 us
    ppermute x13, waiting for transfers between devices, send_cols(): return lax.ppermute(x, 'cols', partners(n_cols, bit))  3.64 us
    convert_element_type x2, other arithmetic, per_device(): u_low, v_low = (own_u.astype(bf16), own_v.astype(bf16))  0.95 us
  transfers between devices with their start and end apart: 18, of which 8 were waited for; matrix products, arithmetic and copies ran while one was open for 0% of the time, Pallas kernels for 8%

profile of v1, /device:TPU:0, one launch (start us, length us, event | category | flops | bytes accessed | tf_op | source)
XLA Modules:
  0.0 37.8 jit_solution(18231537143730861799)
XLA Ops:
  0.6 0.9 %bitcast_convert_fusion.1.refs_3_ = bf16[256,128]{1,0:T(8,128)(2,1)S(1)} fusion(f32[1,256,128]{2,1,0:T(8,128)} %param.5), kind=kLoop, calls=%fused_computation.1 | loop fusion | flops 32768 | bytes 196608 | tf_op jit(solution)/shard_map/convert_element_type | solution.py:245
  1.6 3.1 %collective-permute-start.2 = (bf16[256,128]{1,0:T(8,128)(2,1)S(1)}, bf16[256,128]{1,0:T(8,128)(2,1)S(1)}, u32[]{:S(2)}, u32[]{:S(2)}) collective-permute-start(bf16[256,128]{1,0:T(8,128)(2,1)S(1)} %bitcast_convert_fusion.1.refs_3_), channel_id=1, source_target_pairs={{0,2},{1,3},{2,0},{3,1},{4,6},{5,7},{6,4},{7,5},{8,10},{9,11},{10,... | collective-permute-start | bytes 196616 | tf_op jit(solution)/shard_map/ppermute | solution.py:239
  4.6 2.5 %collective-permute-start.1 = (bf16[256,128]{1,0:T(8,128)(2,1)S(1)}, bf16[256,128]{1,0:T(8,128)(2,1)S(1)}, u32[]{:S(2)}, u32[]{:S(2)}) collective-permute-start(bf16[256,128]{1,0:T(8,128)(2,1)S(1)} %bitcast_convert_fusion.1.refs_3_), channel_id=1, source_target_pairs={{0,6},{1,7},{2,4},{3,5},{4,2},{5,3},{6,0},{7,1},{8,14},{9,15},{10,... | collective-permute-start | bytes 196616 | tf_op jit(solution)/shard_map/ppermute | solution.py:239
  7.1 0.1 collective-permute-start
  7.2 1.6 %collective-permute-start.3 = (bf16[128,128]{1,0:T(8,128)(2,1)S(1)}, bf16[128,128]{1,0:T(8,128)(2,1)S(1)}, u32[]{:S(2)}, u32[]{:S(2)}) collective-permute-start(bf16[128,128]{1,0:T(8,128)(2,1)S(1)} %bitcast_convert_fusion.left), channel_id=1, source_target_pairs={{0,8},{8,0},{16,24},{24,16},{1,9},{9,1},{17,25},{25,17},{2,10},{10... | collective-permute-start | bytes 98312 | tf_op jit(solution)/shard_map/ppermute | solution.py:242
  8.8 2.4 %collective-permute-done.3.right = bf16[128,128]{1,0:T(8,128)(2,1)S(1)} collective-permute-done((bf16[128,128]{1,0:T(8,128)(2,1)S(1)}, bf16[128,128]{1,0:T(8,128)(2,1)S(1)}, u32[]{:S(2)}, u32[]{:S(2)}) %collective-permute-start.3) | collective-permute-done | bytes 32800 | tf_op jit(solution)/shard_map/ppermute | solution.py:242
  11.2 1.5 %collective-permute-start.4 = (bf16[256,128]{1,0:T(8,128)(2,1)S(1)}, bf16[256,128]{1,0:T(8,128)(2,1)S(1)}, u32[]{:S(2)}, u32[]{:S(2)}) collective-permute-start(bf16[256,128]{1,0:T(8,128)(2,1)S(1)} %shard_map.77.refs_7_), channel_id=1, source_target_pairs={{0,16},{8,24},{16,0},{24,8},{1,17},{9,25},{17,1},{25,9},{2,18},{10... | collective-permute-start | bytes 196616 | tf_op jit(solution)/shard_map/ppermute | solution.py:242
  12.8 0.5 %collective-permute-start.8 = (bf16[256,128]{1,0:T(8,128)(2,1)S(1)}, bf16[256,128]{1,0:T(8,128)(2,1)S(1)}, u32[]{:S(2)}, u32[]{:S(2)}) collective-permute-start(bf16[256,128]{1,0:T(8,128)(2,1)S(1)} %collective-permute-done.2.refs_6_), channel_id=1, source_target_pairs={{0,1},{1,0},{2,3},{3,2},{4,5},{5,4},{6,7},{7,6},{8,9},{9,8},{10,11... | collective-permute-start | bytes 196616 | tf_op jit(solution)/shard_map/ppermute | solution.py:239
  13.3 0.1 collective-permute-start.7
  13.3 0.2 collective-permute-done.refs_4_
  13.6 0.2 collective-permute-start.6
  13.8 1.3 %shard_map.76 = (bf16[8,256,256]{2,1,0:T(8,128)(2,1)S(1)}, s32[8,16,256]{2,1,0:T(8,128)S(1)}, s32[8]{0:T(128)S(1)}) custom-call(bf16[8,256,256]{2,1,0:T(8,128)(2,1)} %bitcast.17, s32[8,16,256]{2,1,0:T(8,128)} %bitcast.18, s32[8]{0:T(128)} %bitcast.20), custom_call_target="tpu_custom_call" | custom-call | tf_op jit(solution)/shard_map/pallas_call | solution.py:38
  15.0 0.5 %collective-permute-done.4.refs_8_ = bf16[256,128]{1,0:T(8,128)(2,1)S(1)} collective-permute-done((bf16[256,128]{1,0:T(8,128)(2,1)S(1)}, bf16[256,128]{1,0:T(8,128)(2,1)S(1)}, u32[]{:S(2)}, u32[]{:S(2)}) %collective-permute-start.4) | collective-permute-done | bytes 65568 | tf_op jit(solution)/shard_map/ppermute | solution.py:242
  15.5 1.0 %shard_map.78 = (bf16[4,256,256]{2,1,0:T(8,128)(2,1)S(1)}, bf16[4,256,128]{2,1,0:T(8,128)(2,1)S(1)}, bf16[512,128]{1,0:T(8,128)(2,1)S(1)}, f32[512,128]{1,0:T(8,128)S(1)}, f32[8,256]{1,0:T(8,128)S(1)}) custom-call(s32[1,8]{1,0:T(1,128)S(1)} %bitcast.15, bf16[8,256,256]{2,1,0:T(8,128)(2,1)S(1)} %get-tuple-element.33.refs_1_, ...), custom_call_target="tpu_custom_call" | custom-call | flops 134217728 | tf_op jit(solution)/shard_map/pallas_call | solution.py:38
  16.6 1.0 %shard_map.79 = (bf16[4,256,256]{2,1,0:T(8,128)(2,1)S(1)}, bf16[4,256,128]{2,1,0:T(8,128)(2,1)S(1)}, f32[128,128]{1,0:T(8,128)S(1)}, bf16[3,128,128]{2,1,0:T(8,128)(2,1)S(1)}, f32[8,128]{1,0:T(8,128)S(1)}) custom-call(s32[1,8]{1,0:T(1,128)S(1)} %bitcast.16, bf16[8,256,256]{2,1,0:T(8,128)(2,1)S(1)} %get-tuple-element.33.refs_1_, ...), custom_call_target="tpu_custom_call" | custom-call | flops 134217728 | tf_op jit(solution)/shard_map/pallas_call | solution.py:38
  17.6 0.4 %shard_map.82 = (bf16[4,256,128]{2,1,0:T(8,128)(2,1)S(1)}, bf16[4,256,128]{2,1,0:T(8,128)(2,1)S(1)}) custom-call(bf16[4,256,256]{2,1,0:T(8,128)(2,1)S(1)} %get-tuple-element.46.low_even, bf16[4,256,256]{2,1,0:T(8,128)(2,1)S(1)} %get-tuple-element.47.low_odd, bf16[4,256,128]{2,1,0:T(8,128)(2,1)S(1)} %get-tuple-element.48.right_even, ...), custom_call_target="tpu_custom_call" | custom-call | flops 134217728 | tf_op jit(solution)/shard_map/pallas_call | solution.py:38
  18.0 0.1 collective-permute-start.14
  18.1 0.5 %collective-permute-start.9 = (f32[8,128]{1,0:T(8,128)S(1)}, f32[8,128]{1,0:T(8,128)S(1)}, u32[]{:S(2)}, u32[]{:S(2)}) collective-permute-start(f32[8,128]{1,0:T(8,128)S(1)} %get-tuple-element.39.loss), channel_id=1, source_target_pairs={{0,1},{1,0},{2,3},{3,2},{4,5},{5,4},{6,7},{7,6},{8,9},{9,8},{10,11... | collective-permute-start | bytes 12296 | tf_op jit(solution)/shard_map/ppermute | solution.py:239
  18.6 1.0 %collective-permute-done.9.loss_other = f32[8,128]{1,0:T(8,128)S(1)} collective-permute-done((f32[8,128]{1,0:T(8,128)S(1)}, f32[8,128]{1,0:T(8,128)S(1)}, u32[]{:S(2)}, u32[]{:S(2)}) %collective-permute-start.9) | collective-permute-done | bytes 4128 | tf_op jit(solution)/shard_map/ppermute | solution.py:239
  19.6 1.6 %collective-permute-start.10 = (bf16[144,128]{1,0:T(8,128)(2,1)S(1)}, bf16[144,128]{1,0:T(8,128)(2,1)S(1)}, u32[]{:S(2)}, u32[]{:S(2)}) collective-permute-start(bf16[144,128]{1,0:T(8,128)(2,1)S(1)} %get-tuple-element.42), channel_id=1, source_target_pairs={{0,8},{8,0},{16,24},{24,16},{1,9},{9,1},{17,25},{25,17},{2,10},{10... | collective-permute-start | bytes 110600 | tf_op jit(solution)/shard_map/ppermute | solution.py:242
  21.2 1.5 %collective-permute-start.11 = (bf16[144,128]{1,0:T(8,128)(2,1)S(1)}, bf16[144,128]{1,0:T(8,128)(2,1)S(1)}, u32[]{:S(2)}, u32[]{:S(2)}) collective-permute-start(bf16[144,128]{1,0:T(8,128)(2,1)S(1)} %get-tuple-element.43), channel_id=1, source_target_pairs={{0,16},{8,24},{16,0},{24,8},{1,17},{9,25},{17,1},{25,9},{2,18},{10... | collective-permute-start | bytes 110600 | tf_op jit(solution)/shard_map/ppermute | solution.py:242
  22.7 0.5 %collective-permute-start.12 = (bf16[144,128]{1,0:T(8,128)(2,1)S(1)}, bf16[144,128]{1,0:T(8,128)(2,1)S(1)}, u32[]{:S(2)}, u32[]{:S(2)}) collective-permute-start(bf16[144,128]{1,0:T(8,128)(2,1)S(1)} %get-tuple-element.44), channel_id=1, source_target_pairs={{0,24},{8,16},{16,8},{24,0},{1,25},{9,17},{17,9},{25,1},{2,26},{10... | collective-permute-start | bytes 110600 | tf_op jit(solution)/shard_map/ppermute | solution.py:242
  23.2 0.5 %collective-permute-done.10.refs_0_ = bf16[144,128]{1,0:T(8,128)(2,1)S(1)} collective-permute-done((bf16[144,128]{1,0:T(8,128)(2,1)S(1)}, bf16[144,128]{1,0:T(8,128)(2,1)S(1)}, u32[]{:S(2)}, u32[]{:S(2)}) %collective-permute-start.10) | collective-permute-done | bytes 36896 | tf_op jit(solution)/shard_map/ppermute | solution.py:242
  23.7 1.5 %collective-permute-done.11.refs_1_ = bf16[144,128]{1,0:T(8,128)(2,1)S(1)} collective-permute-done((bf16[144,128]{1,0:T(8,128)(2,1)S(1)}, bf16[144,128]{1,0:T(8,128)(2,1)S(1)}, u32[]{:S(2)}, u32[]{:S(2)}) %collective-permute-start.11) | collective-permute-done | bytes 36896 | tf_op jit(solution)/shard_map/ppermute | solution.py:242
  25.2 2.4 %collective-permute-done.12.refs_2_ = bf16[144,128]{1,0:T(8,128)(2,1)S(1)} collective-permute-done((bf16[144,128]{1,0:T(8,128)(2,1)S(1)}, bf16[144,128]{1,0:T(8,128)(2,1)S(1)}, u32[]{:S(2)}, u32[]{:S(2)}) %collective-permute-start.12) | collective-permute-done | bytes 36896 | tf_op jit(solution)/shard_map/ppermute | solution.py:242
  27.7 3.0 %collective-permute-start.16 = (bf16[272,128]{1,0:T(8,128)(2,1)S(1)}, bf16[272,128]{1,0:T(8,128)(2,1)S(1)}, u32[]{:S(2)}, u32[]{:S(2)}) collective-permute-start(bf16[272,128]{1,0:T(8,128)(2,1)S(1)} %get-tuple-element.56), channel_id=1, source_target_pairs={{0,6},{1,7},{2,4},{3,5},{4,2},{5,3},{6,0},{7,1},{8,14},{9,15},{10,... | collective-permute-start | bytes 208904 | tf_op jit(solution)/shard_map/ppermute | solution.py:239
  30.7 0.5 %collective-permute-start.17 = (bf16[272,128]{1,0:T(8,128)(2,1)S(1)}, bf16[272,128]{1,0:T(8,128)(2,1)S(1)}, u32[]{:S(2)}, u32[]{:S(2)}) collective-permute-start(bf16[272,128]{1,0:T(8,128)(2,1)S(1)} %get-tuple-element.57), channel_id=1, source_target_pairs={{0,2},{1,3},{2,0},{3,1},{4,6},{5,7},{6,4},{7,5},{8,10},{9,11},{10,... | collective-permute-start | bytes 208904 | tf_op jit(solution)/shard_map/ppermute | solution.py:239
  31.2 1.0 %collective-permute-start.15 = (bf16[256,128]{1,0:T(8,128)(2,1)S(1)}, bf16[256,128]{1,0:T(8,128)(2,1)S(1)}, u32[]{:S(2)}, u32[]{:S(2)}) collective-permute-start(bf16[256,128]{1,0:T(8,128)(2,1)S(1)} %get-tuple-element.53), channel_id=1, source_target_pairs={{0,4},{1,5},{2,6},{3,7},{4,0},{5,1},{6,2},{7,3},{8,12},{9,13},{10,... | collective-permute-start | bytes 196616 | tf_op jit(solution)/shard_map/ppermute | solution.py:239
  32.2 1.9 %collective-permute-start.13 = (f32[8,128]{1,0:T(8,128)S(1)}, f32[8,128]{1,0:T(8,128)S(1)}, u32[]{:S(2)}, u32[]{:S(2)}) collective-permute-start(f32[8,128]{1,0:T(8,128)S(1)} %get-tuple-element.45.loss), channel_id=1, source_target_pairs={{0,4},{1,5},{2,6},{3,7},{4,0},{5,1},{6,2},{7,3},{8,12},{9,13},{10,... | collective-permute-start | bytes 12296 | tf_op jit(solution)/shard_map/ppermute | solution.py:239
  34.1 0.6 %shard_map.86 = f32[128,128]{1,0:T(8,128)} custom-call(f32[128,128]{1,0:T(8,128)S(1)} %bitcast.14, f32[128,128]{1,0:T(8,128)S(1)} %get-tuple-element.59.total), custom_call_target="tpu_custom_call" | custom-call | tf_op jit(solution)/shard_map/pallas_call | solution.py:38
  34.7 2.4 %collective-permute-done.13.refs_0_ = f32[8,128]{1,0:T(8,128)S(1)} collective-permute-done((f32[8,128]{1,0:T(8,128)S(1)}, f32[8,128]{1,0:T(8,128)S(1)}, u32[]{:S(2)}, u32[]{:S(2)}) %collective-permute-start.13) | collective-permute-done | bytes 4128 | tf_op jit(solution)/shard_map/ppermute | solution.py:239
  37.1 0.7 %shard_map.85 = (f32[256,128]{1,0:T(8,128)}, f32[1,1]{1,0:T(1,128)}) custom-call(f32[256,128]{1,0:T(8,128)S(1)} %bitcast.12, f32[8,128]{1,0:T(8,128)S(1)} %get-tuple-element.45.loss, f32[8,128]{1,0:T(8,128)S(1)} %collective-permute-done.13.refs_0_, bf16[256,128]{1,0:T(8,128)(2,1)S(1)} %get-tuple-element.52.refs_1_, ...), custom_call_target="tpu_custom_call" | custom-call | tf_op jit(solution)/shard_map/pallas_call | solution.py:38
  (21 shorter events, 0.2 us)
Async XLA Ops:
  0.6 6.6 %copy-start.1 = (f32[1,128,128]{2,1,0:T(8,128)S(1)}, f32[1,128,128]{2,1,0:T(8,128)}, u32[]{:S(2)}) copy-start(f32[1,128,128]{2,1,0:T(8,128)} %param.6) | copy-start | bytes 196612
  1.6 11.2 %collective-permute-start.2 = (bf16[256,128]{1,0:T(8,128)(2,1)S(1)}, bf16[256,128]{1,0:T(8,128)(2,1)S(1)}, u32[]{:S(2)}, u32[]{:S(2)}) collective-permute-start(bf16[256,128]{1,0:T(8,128)(2,1)S(1)} %bitcast_convert_fusion.1.refs_3_), channel_id=1, source_target_pairs={{0,2},{1,3},{2,0},{3,1},{4,6},{5,7},{6,4},{7,5},{8,10},{9,11},{10,... | collective-permute-start | bytes 196616 | tf_op jit(solution)/shard_map/ppermute | solution.py:239
  4.6 8.6 %collective-permute-start.1 = (bf16[256,128]{1,0:T(8,128)(2,1)S(1)}, bf16[256,128]{1,0:T(8,128)(2,1)S(1)}, u32[]{:S(2)}, u32[]{:S(2)}) collective-permute-start(bf16[256,128]{1,0:T(8,128)(2,1)S(1)} %bitcast_convert_fusion.1.refs_3_), channel_id=1, source_target_pairs={{0,6},{1,7},{2,4},{3,5},{4,2},{5,3},{6,0},{7,1},{8,14},{9,15},{10,... | collective-permute-start | bytes 196616 | tf_op jit(solution)/shard_map/ppermute | solution.py:239
  7.1 6.4 %collective-permute-start = (bf16[256,128]{1,0:T(8,128)(2,1)S(1)}, bf16[256,128]{1,0:T(8,128)(2,1)S(1)}, u32[]{:S(2)}, u32[]{:S(2)}) collective-permute-start(bf16[256,128]{1,0:T(8,128)(2,1)S(1)} %bitcast_convert_fusion.1.refs_3_), channel_id=1, source_target_pairs={{0,4},{1,5},{2,6},{3,7},{4,0},{5,1},{6,2},{7,3},{8,12},{9,13},{10,... | collective-permute-start | bytes 196616 | tf_op jit(solution)/shard_map/ppermute | solution.py:239
  7.2 4.0 %collective-permute-start.3 = (bf16[128,128]{1,0:T(8,128)(2,1)S(1)}, bf16[128,128]{1,0:T(8,128)(2,1)S(1)}, u32[]{:S(2)}, u32[]{:S(2)}) collective-permute-start(bf16[128,128]{1,0:T(8,128)(2,1)S(1)} %bitcast_convert_fusion.left), channel_id=1, source_target_pairs={{0,8},{8,0},{16,24},{24,16},{1,9},{9,1},{17,25},{25,17},{2,10},{10... | collective-permute-start | bytes 98312 | tf_op jit(solution)/shard_map/ppermute | solution.py:242
  11.2 4.3 %collective-permute-start.4 = (bf16[256,128]{1,0:T(8,128)(2,1)S(1)}, bf16[256,128]{1,0:T(8,128)(2,1)S(1)}, u32[]{:S(2)}, u32[]{:S(2)}) collective-permute-start(bf16[256,128]{1,0:T(8,128)(2,1)S(1)} %shard_map.77.refs_7_), channel_id=1, source_target_pairs={{0,16},{8,24},{16,0},{24,8},{1,17},{9,25},{17,1},{25,9},{2,18},{10... | collective-permute-start | bytes 196616 | tf_op jit(solution)/shard_map/ppermute | solution.py:242
  12.7 3.8 %collective-permute-start.5 = (bf16[256,128]{1,0:T(8,128)(2,1)S(1)}, bf16[256,128]{1,0:T(8,128)(2,1)S(1)}, u32[]{:S(2)}, u32[]{:S(2)}) collective-permute-start(bf16[256,128]{1,0:T(8,128)(2,1)S(1)} %bitcast_convert_fusion.1.refs_3_), channel_id=1, source_target_pairs={{0,1},{1,0},{2,3},{3,2},{4,5},{5,4},{6,7},{7,6},{8,9},{9,8},{10,11... | collective-permute-start | bytes 196616 | tf_op jit(solution)/shard_map/ppermute | solution.py:239
  12.8 3.8 %collective-permute-start.8 = (bf16[256,128]{1,0:T(8,128)(2,1)S(1)}, bf16[256,128]{1,0:T(8,128)(2,1)S(1)}, u32[]{:S(2)}, u32[]{:S(2)}) collective-permute-start(bf16[256,128]{1,0:T(8,128)(2,1)S(1)} %collective-permute-done.2.refs_6_), channel_id=1, source_target_pairs={{0,1},{1,0},{2,3},{3,2},{4,5},{5,4},{6,7},{7,6},{8,9},{9,8},{10,11... | collective-permute-start | bytes 196616 | tf_op jit(solution)/shard_map/ppermute | solution.py:239
  13.3 3.3 %collective-permute-start.7 = (bf16[256,128]{1,0:T(8,128)(2,1)S(1)}, bf16[256,128]{1,0:T(8,128)(2,1)S(1)}, u32[]{:S(2)}, u32[]{:S(2)}) collective-permute-start(bf16[256,128]{1,0:T(8,128)(2,1)S(1)} %collective-permute-done.1.refs_5_), channel_id=1, source_target_pairs={{0,1},{1,0},{2,3},{3,2},{4,5},{5,4},{6,7},{7,6},{8,9},{9,8},{10,11... | collective-permute-start | bytes 196616 | tf_op jit(solution)/shard_map/ppermute | solution.py:239
  13.6 3.0 %collective-permute-start.6 = (bf16[256,128]{1,0:T(8,128)(2,1)S(1)}, bf16[256,128]{1,0:T(8,128)(2,1)S(1)}, u32[]{:S(2)}, u32[]{:S(2)}) collective-permute-start(bf16[256,128]{1,0:T(8,128)(2,1)S(1)} %collective-permute-done.refs_4_), channel_id=1, source_target_pairs={{0,1},{1,0},{2,3},{3,2},{4,5},{5,4},{6,7},{7,6},{8,9},{9,8},{10,11... | collective-permute-start | bytes 196616 | tf_op jit(solution)/shard_map/ppermute | solution.py:239
  15.5 1.1 %copy-start = (f32[1,256,128]{2,1,0:T(8,128)S(1)}, f32[1,256,128]{2,1,0:T(8,128)}, u32[]{:S(2)}) copy-start(f32[1,256,128]{2,1,0:T(8,128)} %param.5) | copy-start | bytes 393220
  18.0 9.6 %collective-permute-start.14 = (bf16[4,256,128]{2,1,0:T(8,128)(2,1)S(1)}, bf16[4,256,128]{2,1,0:T(8,128)(2,1)S(1)}, u32[]{:S(2)}, u32[]{:S(2)}) collective-permute-start(bf16[4,256,128]{2,1,0:T(8,128)(2,1)S(1)} %get-tuple-element.51), channel_id=1, source_target_pairs={{0,1},{1,0},{2,3},{3,2},{4,5},{5,4},{6,7},{7,6},{8,9},{9,8},{10,11... | collective-permute-start | bytes 786440 | tf_op jit(solution)/shard_map/ppermute | solution.py:239
  18.1 1.5 %collective-permute-start.9 = (f32[8,128]{1,0:T(8,128)S(1)}, f32[8,128]{1,0:T(8,128)S(1)}, u32[]{:S(2)}, u32[]{:S(2)}) collective-permute-start(f32[8,128]{1,0:T(8,128)S(1)} %get-tuple-element.39.loss), channel_id=1, source_target_pairs={{0,1},{1,0},{2,3},{3,2},{4,5},{5,4},{6,7},{7,6},{8,9},{9,8},{10,11... | collective-permute-start | bytes 12296 | tf_op jit(solution)/shard_map/ppermute | solution.py:239
  19.6 4.0 %collective-permute-start.10 = (bf16[144,128]{1,0:T(8,128)(2,1)S(1)}, bf16[144,128]{1,0:T(8,128)(2,1)S(1)}, u32[]{:S(2)}, u32[]{:S(2)}) collective-permute-start(bf16[144,128]{1,0:T(8,128)(2,1)S(1)} %get-tuple-element.42), channel_id=1, source_target_pairs={{0,8},{8,0},{16,24},{24,16},{1,9},{9,1},{17,25},{25,17},{2,10},{10... | collective-permute-start | bytes 110600 | tf_op jit(solution)/shard_map/ppermute | solution.py:242
  21.2 4.0 %collective-permute-start.11 = (bf16[144,128]{1,0:T(8,128)(2,1)S(1)}, bf16[144,128]{1,0:T(8,128)(2,1)S(1)}, u32[]{:S(2)}, u32[]{:S(2)}) collective-permute-start(bf16[144,128]{1,0:T(8,128)(2,1)S(1)} %get-tuple-element.43), channel_id=1, source_target_pairs={{0,16},{8,24},{16,0},{24,8},{1,17},{9,25},{17,1},{25,9},{2,18},{10... | collective-permute-start | bytes 110600 | tf_op jit(solution)/shard_map/ppermute | solution.py:242
  22.7 4.9 %collective-permute-start.12 = (bf16[144,128]{1,0:T(8,128)(2,1)S(1)}, bf16[144,128]{1,0:T(8,128)(2,1)S(1)}, u32[]{:S(2)}, u32[]{:S(2)}) collective-permute-start(bf16[144,128]{1,0:T(8,128)(2,1)S(1)} %get-tuple-element.44), channel_id=1, source_target_pairs={{0,24},{8,16},{16,8},{24,0},{1,25},{9,17},{17,9},{25,1},{2,26},{10... | collective-permute-start | bytes 110600 | tf_op jit(solution)/shard_map/ppermute | solution.py:242
  27.7 9.4 %collective-permute-start.16 = (bf16[272,128]{1,0:T(8,128)(2,1)S(1)}, bf16[272,128]{1,0:T(8,128)(2,1)S(1)}, u32[]{:S(2)}, u32[]{:S(2)}) collective-permute-start(bf16[272,128]{1,0:T(8,128)(2,1)S(1)} %get-tuple-element.56), channel_id=1, source_target_pairs={{0,6},{1,7},{2,4},{3,5},{4,2},{5,3},{6,0},{7,1},{8,14},{9,15},{10,... | collective-permute-start | bytes 208904 | tf_op jit(solution)/shard_map/ppermute | solution.py:239
  30.7 6.4 %collective-permute-start.17 = (bf16[272,128]{1,0:T(8,128)(2,1)S(1)}, bf16[272,128]{1,0:T(8,128)(2,1)S(1)}, u32[]{:S(2)}, u32[]{:S(2)}) collective-permute-start(bf16[272,128]{1,0:T(8,128)(2,1)S(1)} %get-tuple-element.57), channel_id=1, source_target_pairs={{0,2},{1,3},{2,0},{3,1},{4,6},{5,7},{6,4},{7,5},{8,10},{9,11},{10,... | collective-permute-start | bytes 208904 | tf_op jit(solution)/shard_map/ppermute | solution.py:239
  31.2 5.9 %collective-permute-start.15 = (bf16[256,128]{1,0:T(8,128)(2,1)S(1)}, bf16[256,128]{1,0:T(8,128)(2,1)S(1)}, u32[]{:S(2)}, u32[]{:S(2)}) collective-permute-start(bf16[256,128]{1,0:T(8,128)(2,1)S(1)} %get-tuple-element.53), channel_id=1, source_target_pairs={{0,4},{1,5},{2,6},{3,7},{4,0},{5,1},{6,2},{7,3},{8,12},{9,13},{10,... | collective-permute-start | bytes 196616 | tf_op jit(solution)/shard_map/ppermute | solution.py:239
  32.2 4.9 %collective-permute-start.13 = (f32[8,128]{1,0:T(8,128)S(1)}, f32[8,128]{1,0:T(8,128)S(1)}, u32[]{:S(2)}, u32[]{:S(2)}) collective-permute-start(f32[8,128]{1,0:T(8,128)S(1)} %get-tuple-element.45.loss), channel_id=1, source_target_pairs={{0,4},{1,5},{2,6},{3,7},{4,0},{5,1},{6,2},{7,3},{8,12},{9,13},{10,... | collective-permute-start | bytes 12296 | tf_op jit(solution)/shard_map/ppermute | solution.py:239

commit v2 on v1

--- a/solution.py
+++ b/solution.py
@@ -15,7 +15,6 @@
 LOSS_ROWS = 16
 WORD_BITS = 16
 PLAIN = 1
-CROSS = 0
 VMEM_LIMIT = 24 * 2**20
 sds = jax.ShapeDtypeStruct
 
@@ -29,7 +28,7 @@
 
 
 def far_order(n_cols):
-    return [q ^ CROSS for q in sorted(range(2, n_cols, 2), key=lambda q: (q != 4, -q))]
+    return sorted(range(2, n_cols, 2), key=lambda q: (q != 4, -q))
 
 
 def call(body, out_shape, args, scratch=(), spaces=None, flops=0):
@@ -61,16 +60,45 @@
     return rows[0:1] + rows[1:2] + rows[2:3]
 
 
-def fetch_kernel(*refs):
-    count = len(refs) // 2
-    sems = refs[-1]
+def low_kernel(u_hbm, v_hbm, u_own, v_own, u_low, v_low, sems):
+    rows = u_hbm.shape[0] // 2
     copies = [
-        pltpu.make_async_copy(refs[i], refs[count + i], sems.at[i]) for i in range(count)
+        pltpu.make_async_copy(u_hbm.at[:rows], u_own.at[:rows], sems.at[0]),
+        pltpu.make_async_copy(u_hbm.at[rows:], u_own.at[rows:], sems.at[1]),
+        pltpu.make_async_copy(v_hbm, v_own, sems.at[2]),
     ]
     for copy in copies:
         copy.start()
+    copies[0].wait()
+    u_low[:rows, :] = u_own[:rows, :].astype(bf16)
+    copies[1].wait()
+    u_low[rows:, :] = u_own[rows:, :].astype(bf16)
+    copies[2].wait()
+    v_low[...] = v_own[...].astype(bf16)
+
+
+def decode_kernel(values_hbm, words_hbm, ids_hbm, seen, marked, ids, values, words, sems):
+    slots, tile = values.shape[0], values.shape[1]
+    copies = [
+        pltpu.make_async_copy(words_hbm, words, sems.at[slots]),
+        pltpu.make_async_copy(ids_hbm, ids, sems.at[slots + 1]),
+    ]
+    copies += [
+        pltpu.make_async_copy(values_hbm.at[s], values.at[s], sems.at[s]) for s in range(slots)
+    ]
     for copy in copies:
-        copy.wait()
+        copy.start()
+    copies[0].wait()
+    bit = jnp.left_shift(1, lax.broadcasted_iota(jnp.int32, (WORD_BITS, tile), 0))
+    for s in range(slots):
+        copies[2 + s].wait()
+        for w in range(tile // WORD_BITS):
+            rows = slice(w * WORD_BITS, (w + 1) * WORD_BITS)
+            marks = jnp.broadcast_to(words[s, w : w + 1, :], (WORD_BITS, tile))
+            hit = jnp.bitwise_and(marks, bit) != 0
+            seen[s, rows, :] = jnp.where(hit, 1.0, 0.0)
+            marked[s, rows, :] = jnp.where(hit, values[s, rows, :].astype(f32), 0.0)
+    copies[1].wait()
 
 
 def stack_kernel(left, right, out):
@@ -79,49 +107,55 @@
     out[rows:, :] = right[...]
 
 
-def column_of(column_ids, slot):
-    places = lax.broadcasted_iota(jnp.int32, column_ids.shape, 1)
-    picked = jnp.where(places == slot, column_ids[...].astype(f32), 0.0)
-    return jnp.sum(picked).astype(jnp.int32)
-
-
-def tile_slots(places, tile, column_ids, values, words, u_blocks, v_band, low_out, right_out, v_total):
+def column_starts(places, tiles, tile, column_ids):
     col = lax.axis_index("cols")
-    bit = jnp.left_shift(1, lax.broadcasted_iota(jnp.int32, (WORD_BITS, tile), 0))
+    ids = column_ids[...].astype(f32)
+    lanes = lax.broadcasted_iota(jnp.int32, ids.shape, 1)
+    slots = [(col ^ q) * tiles + t for q in places for t in range(tiles)]
+    picked = [jnp.sum(jnp.where(lanes == slot, ids, 0.0)) for slot in slots]
+    return slots, [x.astype(jnp.int32) * tile for x in picked]
+
+
+def residuals(slots, seen, marked, u_blocks, right, low_out):
+    tile = low_out.shape[-1]
+    tiles = u_blocks[0].shape[0] // tile
     squares = jnp.zeros((8, tile), f32)
+    for k, slot in enumerate(slots):
+        t = k % tiles
+        predicted = lax.dot_general(
+            u_blocks[k // tiles][t * tile : (t + 1) * tile, :],
+            right[k],
+            (((1,), (1,)), ((), ())),
+            preferred_element_type=f32,
+        )
+        residual = seen[slot] * predicted - marked[slot]
+        squares += jnp.sum((residual * residual).reshape(-1, 8, tile), axis=0)
+        low_out[k] = residual.astype(bf16)
+    return squares
+
+
+def column_grads(starts, low, u_blocks, v_total):
+    tile = low.shape[-1]
     tiles = u_blocks[0].shape[0] // tile
-    for k, q in enumerate(places):
-        for t in range(tiles):
-            slot = (col ^ q) * tiles + t
-            start = column_of(column_ids, slot) * tile
-            left = u_blocks[k][t * tile : (t + 1) * tile, :]
-            right = v_band[pl.ds(start, tile), :]
-            predicted = lax.dot_general(
-                left, right, (((1,), (1,)), ((), ())), preferred_element_type=f32
-            )
-            diff = predicted - values[slot].astype(f32)
-            parts = []
-            for w in range(tile // WORD_BITS):
-                marks = jnp.broadcast_to(words[slot, w : w + 1, :], (WORD_BITS, tile))
-                seen = jnp.bitwise_and(marks, bit) != 0
-                parts.append(jnp.where(seen, diff[w * WORD_BITS : (w + 1) * WORD_BITS, :], 0.0))
-            residual = jnp.concatenate(parts, axis=0)
-            squares += jnp.sum((residual * residual).reshape(-1, 8, tile), axis=0)
-            low = residual.astype(bf16)
-            low_out[k * tiles + t] = low
-            right_out[k * tiles + t] = right
-            v_total[pl.ds(start, tile), :] += lax.dot_general(
-                low, left, (((0,), (0,)), ((), ())), preferred_element_type=f32
-            )
-    return squares
-
-
-def even_kernel(places, order_v, tile, *refs):
-    column_ids, values, words = refs[:3]
-    u_blocks, (v_stack, v_other, low_out, right_out, v_band, v_total, squares) = (
-        refs[3:-7],
-        refs[-7:],
-    )
+    for k, start in enumerate(starts):
+        t = k % tiles
+        v_total[pl.ds(start, tile), :] += lax.dot_general(
+            low[k],
+            u_blocks[k // tiles][t * tile : (t + 1) * tile, :],
+            (((0,), (0,)), ((), ())),
+            preferred_element_type=f32,
+        )
+
+
+def even_kernel(direct, swapped, order_v, tile, *refs):
+    column_ids, seen, marked = refs[:3]
+    u_blocks, (v_stack, v_other, low, right, right_odd, v_total, squares, v_band) = (
+        refs[3:-8],
+        refs[-8:],
+    )
+    tiles = u_blocks[0].shape[0] // tile
+    slots, starts = column_starts(direct, tiles, tile, column_ids)
+    _, starts_odd = column_starts(swapped, tiles, tile, column_ids)
     row = lax.axis_index("rows")
     n_rows = len(order_v)
     v_rows = v_band.shape[0] // n_rows
@@ -132,40 +166,48 @@
             (k % half) * v_rows : (k % half + 1) * v_rows, :
         ]
     v_total[...] = jnp.zeros_like(v_total)
-    squares[...] = tile_slots(
-        places, tile, column_ids, values, words, u_blocks, v_band, low_out, right_out, v_total
-    )
-
-
-def odd_kernel(places, n_rows, tile, *refs):
-    column_ids, values, words, own_u, own_v, v_band, v_start, squares = refs[:8]
-    u_blocks, (low_out, right_out, keep, send, loss_out, v_total) = refs[8:-6], refs[-6:]
-    row = lax.axis_index("rows")
-    v_total[...] = v_start[...]
-    total = squares[...] + tile_slots(
-        places, tile, column_ids, values, words, u_blocks, v_band, low_out, right_out, v_total
-    )
+    for out, places in ((right, starts), (right_odd, starts_odd)):
+        for k, start in enumerate(places):
+            out[k] = v_band[pl.ds(start, tile), :]
+    squares[...] = residuals(slots, seen, marked, u_blocks, right, low)
+    column_grads(starts, low, u_blocks, v_total)
+
+
+def odd_kernel(swapped, tile, *refs):
+    seen, marked, own_u, own_v, right, squares = refs[:6]
+    u_blocks, (low, loss_out) = refs[6:-2], refs[-2:]
+    col = lax.axis_index("cols")
+    tiles = u_blocks[0].shape[0] // tile
+    slots = [(col ^ q) * tiles + t for q in swapped for t in range(tiles)]
+    total = squares[...] + residuals(slots, seen, marked, u_blocks, right, low)
     u_own = own_u[...]
     v_own = own_v[...]
     loss = 0.5 * jnp.sum(total) + 0.5 * ridge_weight * (
         jnp.sum(u_own * u_own) + jnp.sum(v_own * v_own)
     )
     loss_out[...] = jnp.full(loss_out.shape, loss, f32)
-    v_rows = own_v.shape[0]
+
+
+def rows_kernel(low, right, cross):
+    pairs, tile = cross.shape[0], low.shape[1]
+    tiles = low.shape[0] // pairs
+    for k in range(pairs):
+        for t in range(tiles):
+            grad = jnp.dot(low[k * tiles + t], right[k * tiles + t], preferred_element_type=f32)
+            cross[k, t * tile : (t + 1) * tile, :] = grad.astype(bf16)
+
+
+def columns_kernel(swapped, tile, *refs):
+    column_ids, low, v_start = refs[:3]
+    u_blocks, (keep, send, v_total) = refs[3:-3], refs[-3:]
+    row = lax.axis_index("rows")
+    _, starts = column_starts(swapped, u_blocks[0].shape[0] // tile, tile, column_ids)
+    v_total[...] = v_start[...]
+    column_grads(starts, low, u_blocks, v_total)
+    v_rows = keep.shape[0]
     keep[...] = v_total[pl.ds(row * v_rows, v_rows), :]
-    for q in range(1, n_rows):
+    for q in range(1, send.shape[0] + 1):
         send[q - 1] = v_total[pl.ds((row ^ q) * v_rows, v_rows), :].astype(bf16)
-
-
-def rows_kernel(low_even, low_odd, right_even, right_odd, same, cross):
-    pairs, tile = same.shape[0], low_even.shape[1]
-    tiles = low_even.shape[0] // pairs
-    for low, right, target in ((low_odd, right_odd, cross), (low_even, right_even, same)):
-        for k in range(pairs):
-            for t in range(tiles):
-                slot = k * tiles + t
-                grad = jnp.dot(low[slot], right[slot], preferred_element_type=f32)
-                target[k, t * tile : (t + 1) * tile, :] = grad.astype(bf16)
 
 
 def pack_kernel(loss, loss_other, blocks, *outs):
@@ -187,9 +229,14 @@
         out[rows:, :] = packed
 
 
-def pair_kernel(same, got, *outs):
-    for q, out in enumerate(outs):
-        out[...] = (same[q].astype(f32) + got[q].astype(f32)).astype(bf16)
+def pair_kernel(places, low, right, got, *outs):
+    tile = low.shape[1]
+    tiles = low.shape[0] // got.shape[0]
+    for k, out in zip(places, outs):
+        for t in range(tiles):
+            rows = slice(t * tile, (t + 1) * tile)
+            grad = jnp.dot(low[k * tiles + t], right[k * tiles + t], preferred_element_type=f32)
+            out[rows, :] = (grad + got[k, rows, :].astype(f32)).astype(bf16)
 
 
 def fold_kernel(keep, loss, *refs):
@@ -241,14 +288,25 @@
     def send_rows(x, bit):
         return lax.ppermute(x, "rows", partners(n_rows, bit))
 
-    own_u, own_v = factor_u[0], factor_v[0]
-    u_low, v_low = own_u.astype(bf16), own_v.astype(bf16)
+    block_f32, own_f32 = sds((block_rows, rank), f32), sds((v_rows, rank), f32)
+    own_u, own_v, u_low, v_low = call(
+        low_kernel,
+        (block_f32, own_f32, sds((block_rows, rank), bf16), sds((v_rows, rank), bf16)),
+        tuple(pltpu.with_memory_space_constraint(x[0], pltpu.HBM) for x in (factor_u, factor_v)),
+        [pltpu.SemaphoreType.DMA((3,))],
+        {0: pltpu.HBM, 1: pltpu.HBM},
+    )
     held = (values[0, 0], mask_words[0, 0], tile_cols[0, 0])
-    tile_values, words, column_ids = call(
-        fetch_kernel,
-        tuple(sds(x.shape, x.dtype) for x in held),
+    full = sds((slots, tile, tile), f32)
+    seen, marked, column_ids = call(
+        decode_kernel,
+        (full, full, sds(held[2].shape, jnp.int32)),
         tuple(pltpu.with_memory_space_constraint(x, pltpu.HBM) for x in held),
-        [pltpu.SemaphoreType.DMA((len(held),))],
+        [
+            pltpu.VMEM(held[0].shape, held[0].dtype),
+            pltpu.VMEM(held[1].shape, held[1].dtype),
+            pltpu.SemaphoreType.DMA((slots + 2,)),
+        ],
         {i: pltpu.HBM for i in range(len(held))},
     )
     column_ids = column_ids.reshape(1, slots)
@@ -270,55 +328,62 @@
     right_shape = sds((slots // 2, tile, rank), bf16)
     band = (n_rows * v_rows, rank)
     tile_flops = 2 * slots * tile * tile * rank
-    low_even, right_even, v_band, v_start, squares = call(
-        functools.partial(even_kernel, direct, order_v, tile),
-        (low_shape, right_shape, sds(band, bf16), sds(band, f32), sds((8, tile), f32)),
+    part = sds((pairs, block_rows, rank), bf16)
+    low_even, right_even, right_odd, v_start, squares = call(
+        functools.partial(even_kernel, direct, swapped, order_v, tile),
+        (low_shape, right_shape, right_shape, sds(band, f32), sds((8, tile), f32)),
         (
             column_ids,
-            tile_values,
-            words,
+            seen,
+            marked,
             *[u_blocks[q] for q in direct],
             v_stack,
             v_other,
         ),
+        [pltpu.VMEM(band, bf16)],
         flops=tile_flops,
     )
-    low_odd, right_odd, keep, send, loss = call(
-        functools.partial(odd_kernel, swapped, n_rows, tile),
+    low_odd, loss = call(
+        functools.partial(odd_kernel, swapped, tile),
+        (low_shape, sds((8, rank), f32)),
         (
-            low_shape,
-            right_shape,
-            sds((v_rows, rank), f32),
-            sds((n_rows - 1, v_rows, rank), bf16),
-            sds((8, rank), f32),
-        ),
-        (
-            column_ids,
-            tile_values,
-            words,
+            seen,
+            marked,
             own_u,
             own_v,
-            v_band,
-            v_start,
+            right_odd,
             squares,
             *[u_blocks[q] for q in swapped],
         ),
+        flops=tile_flops,
+    )
+    loss_other = send_cols(loss, 1)
+    cross = call(rows_kernel, part, (low_odd, right_odd), flops=tile_flops)
+    got = send_cols(cross, 1)
+    keep, send = call(
+        functools.partial(columns_kernel, swapped, tile),
+        (sds((v_rows, rank), f32), sds((n_rows - 1, v_rows, rank), bf16)),
+        (column_ids, low_odd, v_start, *[u_blocks[q] for q in swapped]),
         [pltpu.VMEM(band, f32)],
         flops=tile_flops,
     )
-    loss_other = send_cols(loss, 1)
-    part = sds((pairs, block_rows, rank), bf16)
-    same, cross = call(
-        rows_kernel, (part, part), (low_even, low_odd, right_even, right_odd), flops=tile_flops
-    )
-    got = send_cols(cross, 1)
     loss_shape = sds((8, rank), f32)
     share = sds((v_rows + LOSS_ROWS, rank), bf16)
     *shares, loss = call(
         pack_kernel, (share,) * (n_rows - 1) + (loss_shape,), (loss, loss_other, send)
     )
     block = sds((block_rows, rank), bf16)
-    sums = call(pair_kernel, (block,) * pairs, (same, got))
+    first = list(range(1, 1 + PLAIN))
+    rest = [0] + list(range(1 + PLAIN, pairs))
+    sums = {}
+    for places in (first, rest):
+        outs = call(
+            functools.partial(pair_kernel, places),
+            (block,) * len(places),
+            (low_even, right_even, got),
+            flops=tile_flops // pairs,
+        )
+        sums.update(zip(places, outs))
     plain, carrying = far[:PLAIN], far[PLAIN:]
     u_got = [send_cols(sums[direct.index(q)], q) for q in plain]
     v_got = [send_rows(x, q) for q, x in enumerate(shares, 1)]

time: 38 us -> 37.5 us (0.987)
  Pallas kernels: 5.2 us -> 6.24 us
  other arithmetic: 0.95 us -> 0 us
  waiting for transfers between devices: 10.9 us -> 10.4 us
    pallas_call x11 -> x14, Pallas kernels: 5.2 us -> 6.24 us  [call(): pl.pallas_call(body, out_shape=out_shape, in_specs=specs, out_specs=jax.t...]
    convert_element_type x2 -> x0, other arithmetic: 0.95 us -> none  [per_device(): u_low, v_low = (own_u.astype(bf16), own_v.astype(bf16))]
  transfers between devices with their start and end apart: 18 -> 18, of which waited for: 8 -> 8; matrix products, arithmetic and copies ran while one was open for 0% -> 0% of each run, Pallas kernels for 8% -> 9%
where the time goes in v2:
time: 37.5 us; the launch traced here: 37.4 us
  starting transfers between devices  20 us (53%)
  waiting for transfers between devices  10.4 us (28%)
  Pallas kernels  6.24 us (17%)
  between operations  0.75 us (2%)
    ppermute x13, starting transfers between devices, send_cols(): return lax.ppermute(x, 'cols', partners(n_cols, bit))  13.4 us
    ppermute x5, waiting for transfers between devices, send_rows(): return lax.ppermute(x, 'rows', partners(n_rows, bit))  7.01 us
    ppermute x5, starting transfers between devices, send_rows(): return lax.ppermute(x, 'rows', partners(n_rows, bit))  6.56 us
    pallas_call x14, Pallas kernels, call(): pl.pallas_call(body, out_shape=out_shape, in_specs=specs, out_specs=jax.t...  6.24 us
    ppermute x13, waiting for transfers between devices, send_cols(): return lax.ppermute(x, 'cols', partners(n_cols, bit))  3.35 us
  transfers between devices with their start and end apart: 18, of which 8 were waited for; matrix products, arithmetic and copies ran while one was open for 0% of the time, Pallas kernels for 9%

profile of v2, /device:TPU:0, one launch (start us, length us, event | category | flops | bytes accessed | tf_op | source)
XLA Modules:
  0.0 37.4 jit_solution(6055796201415206521)
XLA Ops:
  0.6 0.9 %shard_map.76 = (f32[256,128]{1,0:T(8,128)S(1)}, f32[128,128]{1,0:T(8,128)S(1)}, bf16[256,128]{1,0:T(8,128)(2,1)S(1)}, bf16[128,128]{1,0:T(8,128)(2,1)S(1)}) custom-call(f32[256,128]{1,0:T(8,128)} %bitcast.13, f32[128,128]{1,0:T(8,128)} %bitcast.14), custom_call_target="tpu_custom_call" | custom-call | tf_op jit(solution)/shard_map/pallas_call | solution.py:37
  1.6 3.1 %collective-permute-start.2 = (bf16[256,128]{1,0:T(8,128)(2,1)S(1)}, bf16[256,128]{1,0:T(8,128)(2,1)S(1)}, u32[]{:S(2)}, u32[]{:S(2)}) collective-permute-start(bf16[256,128]{1,0:T(8,128)(2,1)S(1)} %get-tuple-element.37.refs_3_), channel_id=1, source_target_pairs={{0,2},{1,3},{2,0},{3,1},{4,6},{5,7},{6,4},{7,5},{8,10},{9,11},{10,... | collective-permute-start | bytes 196616 | tf_op jit(solution)/shard_map/ppermute | solution.py:286
  4.7 2.5 %collective-permute-start.1 = (bf16[256,128]{1,0:T(8,128)(2,1)S(1)}, bf16[256,128]{1,0:T(8,128)(2,1)S(1)}, u32[]{:S(2)}, u32[]{:S(2)}) collective-permute-start(bf16[256,128]{1,0:T(8,128)(2,1)S(1)} %get-tuple-element.37.refs_3_), channel_id=1, source_target_pairs={{0,6},{1,7},{2,4},{3,5},{4,2},{5,3},{6,0},{7,1},{8,14},{9,15},{10,... | collective-permute-start | bytes 196616 | tf_op jit(solution)/shard_map/ppermute | solution.py:286
  7.3 1.5 %collective-permute-start.3 = (bf16[128,128]{1,0:T(8,128)(2,1)S(1)}, bf16[128,128]{1,0:T(8,128)(2,1)S(1)}, u32[]{:S(2)}, u32[]{:S(2)}) collective-permute-start(bf16[128,128]{1,0:T(8,128)(2,1)S(1)} %get-tuple-element.38.left), channel_id=1, source_target_pairs={{0,8},{8,0},{16,24},{24,16},{1,9},{9,1},{17,25},{25,17},{2,10},{10... | collective-permute-start | bytes 98312 | tf_op jit(solution)/shard_map/ppermute | solution.py:289
  8.8 2.4 %collective-permute-done.3.right = bf16[128,128]{1,0:T(8,128)(2,1)S(1)} collective-permute-done((bf16[128,128]{1,0:T(8,128)(2,1)S(1)}, bf16[128,128]{1,0:T(8,128)(2,1)S(1)}, u32[]{:S(2)}, u32[]{:S(2)}) %collective-permute-start.3) | collective-permute-done | bytes 32800 | tf_op jit(solution)/shard_map/ppermute | solution.py:289
  11.2 1.5 %collective-permute-start.4 = (bf16[256,128]{1,0:T(8,128)(2,1)S(1)}, bf16[256,128]{1,0:T(8,128)(2,1)S(1)}, u32[]{:S(2)}, u32[]{:S(2)}) collective-permute-start(bf16[256,128]{1,0:T(8,128)(2,1)S(1)} %shard_map.78.refs_7_), channel_id=1, source_target_pairs={{0,16},{8,24},{16,0},{24,8},{1,17},{9,25},{17,1},{25,9},{2,18},{10... | collective-permute-start | bytes 196616 | tf_op jit(solution)/shard_map/ppermute | solution.py:289
  12.7 0.5 %collective-permute-start.8 = (bf16[256,128]{1,0:T(8,128)(2,1)S(1)}, bf16[256,128]{1,0:T(8,128)(2,1)S(1)}, u32[]{:S(2)}, u32[]{:S(2)}) collective-permute-start(bf16[256,128]{1,0:T(8,128)(2,1)S(1)} %collective-permute-done.2.refs_6_), channel_id=1, source_target_pairs={{0,1},{1,0},{2,3},{3,2},{4,5},{5,4},{6,7},{7,6},{8,9},{9,8},{10,11... | collective-permute-start | bytes 196616 | tf_op jit(solution)/shard_map/ppermute | solution.py:286
  13.3 0.3 collective-permute-done.refs_4_
  13.8 1.5 %shard_map.77 = (f32[8,256,256]{2,1,0:T(8,128)S(1)}, f32[8,256,256]{2,1,0:T(8,128)S(1)}, s32[8]{0:T(128)S(1)}) custom-call(bf16[8,256,256]{2,1,0:T(8,128)(2,1)} %bitcast.11, s32[8,16,256]{2,1,0:T(8,128)} %bitcast.12, s32[8]{0:T(128)} %bitcast.16), custom_call_target="tpu_custom_call" | custom-call | tf_op jit(solution)/shard_map/pallas_call | solution.py:37
  15.3 0.2 collective-permute-done.4.refs_8_
  15.5 0.8 %shard_map.79 = (bf16[4,256,256]{2,1,0:T(8,128)(2,1)S(1)}, bf16[4,256,128]{2,1,0:T(8,128)(2,1)S(1)}, bf16[4,256,128]{2,1,0:T(8,128)(2,1)S(1)}, f32[512,128]{1,0:T(8,128)S(1)}, f32[8,256]{1,0:T(8,128)S(1)}) custom-call(s32[1,8]{1,0:T(1,128)S(1)} %bitcast.9, f32[8,256,256]{2,1,0:T(8,128)S(1)} %get-tuple-element.34.refs_1_.refs_0_, ...), custom_call_target="tpu_custom_call" | custom-call | flops 134217728 | tf_op jit(solution)/shard_map/pallas_call | solution.py:37
  16.3 0.5 %shard_map.80 = (bf16[4,256,256]{2,1,0:T(8,128)(2,1)S(1)}, f32[8,128]{1,0:T(8,128)S(1)}) custom-call(f32[8,256,256]{2,1,0:T(8,128)S(1)} %get-tuple-element.34.refs_1_.refs_0_, f32[8,256,256]{2,1,0:T(8,128)S(1)} %get-tuple-element.35.refs_2_.refs_1_, f32[256,128]{1,0:T(8,128)S(1)} %get-tuple-element.32.refs_2_.own_u, ...), custom_call_target="tpu_custom_call" | custom-call | flops 134217728 | tf_op jit(solution)/shard_map/pallas_call | solution.py:37
  16.8 0.3 shard_map.84
  17.1 0.2 collective-permute-start.14
  17.4 0.3 collective-permute-start.9
  17.7 0.4 shard_map.81
  18.1 0.7 %collective-permute-done.9.loss_other = f32[8,128]{1,0:T(8,128)S(1)} collective-permute-done((f32[8,128]{1,0:T(8,128)S(1)}, f32[8,128]{1,0:T(8,128)S(1)}, u32[]{:S(2)}, u32[]{:S(2)}) %collective-permute-start.9) | collective-permute-done | bytes 4128 | tf_op jit(solution)/shard_map/ppermute | solution.py:286
  18.8 1.6 %collective-permute-start.10 = (bf16[144,128]{1,0:T(8,128)(2,1)S(1)}, bf16[144,128]{1,0:T(8,128)(2,1)S(1)}, u32[]{:S(2)}, u32[]{:S(2)}) collective-permute-start(bf16[144,128]{1,0:T(8,128)(2,1)S(1)} %get-tuple-element.47), channel_id=1, source_target_pairs={{0,8},{8,0},{16,24},{24,16},{1,9},{9,1},{17,25},{25,17},{2,10},{10... | collective-permute-start | bytes 110600 | tf_op jit(solution)/shard_map/ppermute | solution.py:289
  20.3 1.5 %collective-permute-start.11 = (bf16[144,128]{1,0:T(8,128)(2,1)S(1)}, bf16[144,128]{1,0:T(8,128)(2,1)S(1)}, u32[]{:S(2)}, u32[]{:S(2)}) collective-permute-start(bf16[144,128]{1,0:T(8,128)(2,1)S(1)} %get-tuple-element.48), channel_id=1, source_target_pairs={{0,16},{8,24},{16,0},{24,8},{1,17},{9,25},{17,1},{25,9},{2,18},{10... | collective-permute-start | bytes 110600 | tf_op jit(solution)/shard_map/ppermute | solution.py:289
  21.8 0.5 %collective-permute-start.12 = (bf16[144,128]{1,0:T(8,128)(2,1)S(1)}, bf16[144,128]{1,0:T(8,128)(2,1)S(1)}, u32[]{:S(2)}, u32[]{:S(2)}) collective-permute-start(bf16[144,128]{1,0:T(8,128)(2,1)S(1)} %get-tuple-element.49), channel_id=1, source_target_pairs={{0,24},{8,16},{16,8},{24,0},{1,25},{9,17},{17,9},{25,1},{2,26},{10... | collective-permute-start | bytes 110600 | tf_op jit(solution)/shard_map/ppermute | solution.py:289
  22.3 0.5 %collective-permute-done.10.refs_0_ = bf16[144,128]{1,0:T(8,128)(2,1)S(1)} collective-permute-done((bf16[144,128]{1,0:T(8,128)(2,1)S(1)}, bf16[144,128]{1,0:T(8,128)(2,1)S(1)}, u32[]{:S(2)}, u32[]{:S(2)}) %collective-permute-start.10) | collective-permute-done | bytes 36896 | tf_op jit(solution)/shard_map/ppermute | solution.py:289
  22.8 1.5 %collective-permute-done.11.refs_1_ = bf16[144,128]{1,0:T(8,128)(2,1)S(1)} collective-permute-done((bf16[144,128]{1,0:T(8,128)(2,1)S(1)}, bf16[144,128]{1,0:T(8,128)(2,1)S(1)}, u32[]{:S(2)}, u32[]{:S(2)}) %collective-permute-start.11) | collective-permute-done | bytes 36896 | tf_op jit(solution)/shard_map/ppermute | solution.py:289
  24.3 2.4 %collective-permute-done.12.refs_2_ = bf16[144,128]{1,0:T(8,128)(2,1)S(1)} collective-permute-done((bf16[144,128]{1,0:T(8,128)(2,1)S(1)}, bf16[144,128]{1,0:T(8,128)(2,1)S(1)}, u32[]{:S(2)}, u32[]{:S(2)}) %collective-permute-start.12) | collective-permute-done | bytes 36896 | tf_op jit(solution)/shard_map/ppermute | solution.py:289
  26.7 0.2 shard_map.85
  27.0 3.0 %collective-permute-start.16 = (bf16[272,128]{1,0:T(8,128)(2,1)S(1)}, bf16[272,128]{1,0:T(8,128)(2,1)S(1)}, u32[]{:S(2)}, u32[]{:S(2)}) collective-permute-start(bf16[272,128]{1,0:T(8,128)(2,1)S(1)} %get-tuple-element.56), channel_id=1, source_target_pairs={{0,6},{1,7},{2,4},{3,5},{4,2},{5,3},{6,0},{7,1},{8,14},{9,15},{10,... | collective-permute-start | bytes 208904 | tf_op jit(solution)/shard_map/ppermute | solution.py:286
  30.0 0.5 %collective-permute-start.17 = (bf16[272,128]{1,0:T(8,128)(2,1)S(1)}, bf16[272,128]{1,0:T(8,128)(2,1)S(1)}, u32[]{:S(2)}, u32[]{:S(2)}) collective-permute-start(bf16[272,128]{1,0:T(8,128)(2,1)S(1)} %get-tuple-element.57), channel_id=1, source_target_pairs={{0,2},{1,3},{2,0},{3,1},{4,6},{5,7},{6,4},{7,5},{8,10},{9,11},{10,... | collective-permute-start | bytes 208904 | tf_op jit(solution)/shard_map/ppermute | solution.py:286
  30.5 0.2 shard_map.86
  30.6 1.1 %collective-permute-start.15 = (bf16[256,128]{1,0:T(8,128)(2,1)S(1)}, bf16[256,128]{1,0:T(8,128)(2,1)S(1)}, u32[]{:S(2)}, u32[]{:S(2)}) collective-permute-start(bf16[256,128]{1,0:T(8,128)(2,1)S(1)} %shard_map.86), channel_id=1, source_target_pairs={{0,4},{1,5},{2,6},{3,7},{4,0},{5,1},{6,2},{7,3},{8,12},{9,13},{10,... | collective-permute-start | bytes 196616 | tf_op jit(solution)/shard_map/ppermute | solution.py:286
  31.7 1.9 %collective-permute-start.13 = (f32[8,128]{1,0:T(8,128)S(1)}, f32[8,128]{1,0:T(8,128)S(1)}, u32[]{:S(2)}, u32[]{:S(2)}) collective-permute-start(f32[8,128]{1,0:T(8,128)S(1)} %get-tuple-element.50.loss), channel_id=1, source_target_pairs={{0,4},{1,5},{2,6},{3,7},{4,0},{5,1},{6,2},{7,3},{8,12},{9,13},{10,... | collective-permute-start | bytes 12296 | tf_op jit(solution)/shard_map/ppermute | solution.py:286
  33.6 0.6 %shard_map.89 = f32[128,128]{1,0:T(8,128)} custom-call(f32[128,128]{1,0:T(8,128)S(1)} %get-tuple-element.36.refs_3_.own_v, f32[128,128]{1,0:T(8,128)S(1)} %get-tuple-element.59.total), custom_call_target="tpu_custom_call" | custom-call | tf_op jit(solution)/shard_map/pallas_call | solution.py:37
  34.3 2.4 %collective-permute-done.13.refs_0_ = f32[8,128]{1,0:T(8,128)S(1)} collective-permute-done((f32[8,128]{1,0:T(8,128)S(1)}, f32[8,128]{1,0:T(8,128)S(1)}, u32[]{:S(2)}, u32[]{:S(2)}) %collective-permute-start.13) | collective-permute-done | bytes 4128 | tf_op jit(solution)/shard_map/ppermute | solution.py:286
  36.6 0.7 %shard_map.88 = (f32[256,128]{1,0:T(8,128)}, f32[1,1]{1,0:T(1,128)}) custom-call(f32[256,128]{1,0:T(8,128)S(1)} %get-tuple-element.32.refs_2_.own_u, f32[8,128]{1,0:T(8,128)S(1)} %get-tuple-element.50.loss, f32[8,128]{1,0:T(8,128)S(1)} %collective-permute-done.13.refs_0_, bf16[256,128]{1,0:T(8,128)(2,1)S(1)} %get-tuple-element.53.refs_1_, ...), custom_call_target="tpu_custom_call" | custom-call | tf_op jit(solution)/shard_map/pallas_call | solution.py:37
  (18 shorter events, 0.4 us)
Async XLA Ops:
  1.6 11.2 %collective-permute-start.2 = (bf16[256,128]{1,0:T(8,128)(2,1)S(1)}, bf16[256,128]{1,0:T(8,128)(2,1)S(1)}, u32[]{:S(2)}, u32[]{:S(2)}) collective-permute-start(bf16[256,128]{1,0:T(8,128)(2,1)S(1)} %get-tuple-element.37.refs_3_), channel_id=1, source_target_pairs={{0,2},{1,3},{2,0},{3,1},{4,6},{5,7},{6,4},{7,5},{8,10},{9,11},{10,... | collective-permute-start | bytes 196616 | tf_op jit(solution)/shard_map/ppermute | solution.py:286
  4.7 8.6 %collective-permute-start.1 = (bf16[256,128]{1,0:T(8,128)(2,1)S(1)}, bf16[256,128]{1,0:T(8,128)(2,1)S(1)}, u32[]{:S(2)}, u32[]{:S(2)}) collective-permute-start(bf16[256,128]{1,0:T(8,128)(2,1)S(1)} %get-tuple-element.37.refs_3_), channel_id=1, source_target_pairs={{0,6},{1,7},{2,4},{3,5},{4,2},{5,3},{6,0},{7,1},{8,14},{9,15},{10,... | collective-permute-start | bytes 196616 | tf_op jit(solution)/shard_map/ppermute | solution.py:286
  7.2 6.4 %collective-permute-start = (bf16[256,128]{1,0:T(8,128)(2,1)S(1)}, bf16[256,128]{1,0:T(8,128)(2,1)S(1)}, u32[]{:S(2)}, u32[]{:S(2)}) collective-permute-start(bf16[256,128]{1,0:T(8,128)(2,1)S(1)} %get-tuple-element.37.refs_3_), channel_id=1, source_target_pairs={{0,4},{1,5},{2,6},{3,7},{4,0},{5,1},{6,2},{7,3},{8,12},{9,13},{10,... | collective-permute-start | bytes 196616 | tf_op jit(solution)/shard_map/ppermute | solution.py:286
  7.3 3.9 %collective-permute-start.3 = (bf16[128,128]{1,0:T(8,128)(2,1)S(1)}, bf16[128,128]{1,0:T(8,128)(2,1)S(1)}, u32[]{:S(2)}, u32[]{:S(2)}) collective-permute-start(bf16[128,128]{1,0:T(8,128)(2,1)S(1)} %get-tuple-element.38.left), channel_id=1, source_target_pairs={{0,8},{8,0},{16,24},{24,16},{1,9},{9,1},{17,25},{25,17},{2,10},{10... | collective-permute-start | bytes 98312 | tf_op jit(solution)/shard_map/ppermute | solution.py:289
  11.2 4.3 %collective-permute-start.4 = (bf16[256,128]{1,0:T(8,128)(2,1)S(1)}, bf16[256,128]{1,0:T(8,128)(2,1)S(1)}, u32[]{:S(2)}, u32[]{:S(2)}) collective-permute-start(bf16[256,128]{1,0:T(8,128)(2,1)S(1)} %shard_map.78.refs_7_), channel_id=1, source_target_pairs={{0,16},{8,24},{16,0},{24,8},{1,17},{9,25},{17,1},{25,9},{2,18},{10... | collective-permute-start | bytes 196616 | tf_op jit(solution)/shard_map/ppermute | solution.py:289
  12.7 3.5 %collective-permute-start.5 = (bf16[256,128]{1,0:T(8,128)(2,1)S(1)}, bf16[256,128]{1,0:T(8,128)(2,1)S(1)}, u32[]{:S(2)}, u32[]{:S(2)}) collective-permute-start(bf16[256,128]{1,0:T(8,128)(2,1)S(1)} %get-tuple-element.37.refs_3_), channel_id=1, source_target_pairs={{0,1},{1,0},{2,3},{3,2},{4,5},{5,4},{6,7},{7,6},{8,9},{9,8},{10,11... | collective-permute-start | bytes 196616 | tf_op jit(solution)/shard_map/ppermute | solution.py:286
  12.7 3.5 %collective-permute-start.8 = (bf16[256,128]{1,0:T(8,128)(2,1)S(1)}, bf16[256,128]{1,0:T(8,128)(2,1)S(1)}, u32[]{:S(2)}, u32[]{:S(2)}) collective-permute-start(bf16[256,128]{1,0:T(8,128)(2,1)S(1)} %collective-permute-done.2.refs_6_), channel_id=1, source_target_pairs={{0,1},{1,0},{2,3},{3,2},{4,5},{5,4},{6,7},{7,6},{8,9},{9,8},{10,11... | collective-permute-start | bytes 196616 | tf_op jit(solution)/shard_map/ppermute | solution.py:286
  13.2 3.0 %collective-permute-start.7 = (bf16[256,128]{1,0:T(8,128)(2,1)S(1)}, bf16[256,128]{1,0:T(8,128)(2,1)S(1)}, u32[]{:S(2)}, u32[]{:S(2)}) collective-permute-start(bf16[256,128]{1,0:T(8,128)(2,1)S(1)} %collective-permute-done.1.refs_5_), channel_id=1, source_target_pairs={{0,1},{1,0},{2,3},{3,2},{4,5},{5,4},{6,7},{7,6},{8,9},{9,8},{10,11... | collective-permute-start | bytes 196616 | tf_op jit(solution)/shard_map/ppermute | solution.py:286
  13.6 2.7 %collective-permute-start.6 = (bf16[256,128]{1,0:T(8,128)(2,1)S(1)}, bf16[256,128]{1,0:T(8,128)(2,1)S(1)}, u32[]{:S(2)}, u32[]{:S(2)}) collective-permute-start(bf16[256,128]{1,0:T(8,128)(2,1)S(1)} %collective-permute-done.refs_4_), channel_id=1, source_target_pairs={{0,1},{1,0},{2,3},{3,2},{4,5},{5,4},{6,7},{7,6},{8,9},{9,8},{10,11... | collective-permute-start | bytes 196616 | tf_op jit(solution)/shard_map/ppermute | solution.py:286
  17.1 9.6 %collective-permute-start.14 = (bf16[4,256,128]{2,1,0:T(8,128)(2,1)S(1)}, bf16[4,256,128]{2,1,0:T(8,128)(2,1)S(1)}, u32[]{:S(2)}, u32[]{:S(2)}) collective-permute-start(bf16[4,256,128]{2,1,0:T(8,128)(2,1)S(1)} %shard_map.84), channel_id=1, source_target_pairs={{0,1},{1,0},{2,3},{3,2},{4,5},{5,4},{6,7},{7,6},{8,9},{9,8},{10,11... | collective-permute-start | bytes 786440 | tf_op jit(solution)/shard_map/ppermute | solution.py:286
  17.4 1.4 %collective-permute-start.9 = (f32[8,128]{1,0:T(8,128)S(1)}, f32[8,128]{1,0:T(8,128)S(1)}, u32[]{:S(2)}, u32[]{:S(2)}) collective-permute-start(f32[8,128]{1,0:T(8,128)S(1)} %get-tuple-element.44.loss), channel_id=1, source_target_pairs={{0,1},{1,0},{2,3},{3,2},{4,5},{5,4},{6,7},{7,6},{8,9},{9,8},{10,11... | collective-permute-start | bytes 12296 | tf_op jit(solution)/shard_map/ppermute | solution.py:286
  18.8 4.0 %collective-permute-start.10 = (bf16[144,128]{1,0:T(8,128)(2,1)S(1)}, bf16[144,128]{1,0:T(8,128)(2,1)S(1)}, u32[]{:S(2)}, u32[]{:S(2)}) collective-permute-start(bf16[144,128]{1,0:T(8,128)(2,1)S(1)} %get-tuple-element.47), channel_id=1, source_target_pairs={{0,8},{8,0},{16,24},{24,16},{1,9},{9,1},{17,25},{25,17},{2,10},{10... | collective-permute-start | bytes 110600 | tf_op jit(solution)/shard_map/ppermute | solution.py:289
  20.3 4.0 %collective-permute-start.11 = (bf16[144,128]{1,0:T(8,128)(2,1)S(1)}, bf16[144,128]{1,0:T(8,128)(2,1)S(1)}, u32[]{:S(2)}, u32[]{:S(2)}) collective-permute-start(bf16[144,128]{1,0:T(8,128)(2,1)S(1)} %get-tuple-element.48), channel_id=1, source_target_pairs={{0,16},{8,24},{16,0},{24,8},{1,17},{9,25},{17,1},{25,9},{2,18},{10... | collective-permute-start | bytes 110600 | tf_op jit(solution)/shard_map/ppermute | solution.py:289
  21.8 4.9 %collective-permute-start.12 = (bf16[144,128]{1,0:T(8,128)(2,1)S(1)}, bf16[144,128]{1,0:T(8,128)(2,1)S(1)}, u32[]{:S(2)}, u32[]{:S(2)}) collective-permute-start(bf16[144,128]{1,0:T(8,128)(2,1)S(1)} %get-tuple-element.49), channel_id=1, source_target_pairs={{0,24},{8,16},{16,8},{24,0},{1,25},{9,17},{17,9},{25,1},{2,26},{10... | collective-permute-start | bytes 110600 | tf_op jit(solution)/shard_map/ppermute | solution.py:289
  27.0 9.6 %collective-permute-start.16 = (bf16[272,128]{1,0:T(8,128)(2,1)S(1)}, bf16[272,128]{1,0:T(8,128)(2,1)S(1)}, u32[]{:S(2)}, u32[]{:S(2)}) collective-permute-start(bf16[272,128]{1,0:T(8,128)(2,1)S(1)} %get-tuple-element.56), channel_id=1, source_target_pairs={{0,6},{1,7},{2,4},{3,5},{4,2},{5,3},{6,0},{7,1},{8,14},{9,15},{10,... | collective-permute-start | bytes 208904 | tf_op jit(solution)/shard_map/ppermute | solution.py:286
  30.0 6.6 %collective-permute-start.17 = (bf16[272,128]{1,0:T(8,128)(2,1)S(1)}, bf16[272,128]{1,0:T(8,128)(2,1)S(1)}, u32[]{:S(2)}, u32[]{:S(2)}) collective-permute-start(bf16[272,128]{1,0:T(8,128)(2,1)S(1)} %get-tuple-element.57), channel_id=1, source_target_pairs={{0,2},{1,3},{2,0},{3,1},{4,6},{5,7},{6,4},{7,5},{8,10},{9,11},{10,... | collective-permute-start | bytes 208904 | tf_op jit(solution)/shard_map/ppermute | solution.py:286
  30.6 6.0 %collective-permute-start.15 = (bf16[256,128]{1,0:T(8,128)(2,1)S(1)}, bf16[256,128]{1,0:T(8,128)(2,1)S(1)}, u32[]{:S(2)}, u32[]{:S(2)}) collective-permute-start(bf16[256,128]{1,0:T(8,128)(2,1)S(1)} %shard_map.86), channel_id=1, source_target_pairs={{0,4},{1,5},{2,6},{3,7},{4,0},{5,1},{6,2},{7,3},{8,12},{9,13},{10,... | collective-permute-start | bytes 196616 | tf_op jit(solution)/shard_map/ppermute | solution.py:286
  31.7 4.9 %collective-permute-start.13 = (f32[8,128]{1,0:T(8,128)S(1)}, f32[8,128]{1,0:T(8,128)S(1)}, u32[]{:S(2)}, u32[]{:S(2)}) collective-permute-start(f32[8,128]{1,0:T(8,128)S(1)} %get-tuple-element.50.loss), channel_id=1, source_target_pairs={{0,4},{1,5},{2,6},{3,7},{4,0},{5,1},{6,2},{7,3},{8,12},{9,13},{10,... | collective-permute-start | bytes 12296 | tf_op jit(solution)/shard_map/ppermute | solution.py:286
